TPU v7x, 256 devices: a whole 4x4x8 slice. The times are simulated.
256 devices in a mesh: wide: 16 (over x, y), grp: 16 (over z, core).
Axes of the slice: x: 4, y: 4, z: 8, core: 2. Of those that a mesh axis runs over, the one named last changes fastest.
Arguments:
- surf_depth: int32 [16, 16, 16, 4096], P('wide', 'grp'), may hold values from 0 to 1073741823
- surf_color: bfloat16 [16, 16, 16, 3, 4096], P('wide', 'grp'), may hold values from 0 to 2
- surf_box: int32 [16, 16, 16, 4], P('wide', 'grp'), may hold values from 0 to 64, as said below
- vol_color: bfloat16 [16, 16, 16, 8, 3, 4096], P('wide', 'grp'), may hold values from 0 to 4
- vol_alpha: bfloat16 [16, 16, 16, 8, 4096], P('wide', 'grp'), may hold values from 0.0009994507 to 0.039794922
- vol_box: int32 [16, 16, 16, 4], P('wide', 'grp'), may hold values from 0 to 64, as said below
- ray_entry: int32 [16, 16, 16, 4096], P('wide', 'grp'), may hold values from 0 to 939524095
- ray_step: int32 [16, 16, 16, 4096], P('wide', 'grp'), may hold values from 1048576 to 16777215
- order: int32 [16, 16], P('grp'), may hold values from 0 to 15, each once within a row
Outputs:
- frame: float32 [16, 16, 4, 4096], P('grp', 'wide')
Inputs may be any that keep to these rules, and one draw needn't show every extreme that they name: `surf_box`: each box gives rows [top, bottom) and columns [left, right) of a tile with 1 to 16 rows and 1 or more columns; in every draw one tile row has boxes of exactly 16 rows from every source, and other tiles reach it too. `vol_box`: each box gives rows [top, bottom) and columns [left, right) of a tile with 1 to 32 rows and 1 or more columns; in every draw one tile column has boxes of exactly 32 rows from every brick of every band, and other tiles reach it too. `order`: each row is a permutation of 0 .. 15.
All inputs are finite; a program needn't handle non-finite values.
Results may differ from a plain program's by a relative error of at most 0.0003.
Values may be sent and summed in bfloat16 or wider, within the bound.
A program may use at most 64 MiB of HBM per device.

v0:
```python
import jax
import jax.numpy as jnp
from jax import lax
from jax.sharding import Mesh
from jax.sharding import PartitionSpec as P

TILE_H = 64
TILE_W = 64
GRP = ("grp_0", "grp_1")


far_depth = 1073741824


def sent_to_all(array, axis):
    copies = jnp.broadcast_to(array, (lax.axis_size(axis), *array.shape))
    return lax.all_to_all(copies, axis, split_axis=0, concat_axis=0, tiled=True)


def in_order(pieces, dim):
    shape = list(pieces.shape[1:])
    shape[dim] *= pieces.shape[0]
    return jnp.moveaxis(pieces, 0, dim).reshape(shape)


def gathered_copies(array, axis, dim):
    pieces = sent_to_all(array, axis)
    return in_order(pieces, dim)


def split_up(array, dim, size):
    before, after = (array.shape[:dim], array.shape[dim + 1 :])
    return jnp.moveaxis(array.reshape(*before, size, -1, *after), dim, 0)


def turned_blocks(pieces, axes, turns):
    inside = pieces.shape[1:]
    result = pieces.reshape(*(lax.axis_size(a) for a in axes), *inside)
    for k in turns:
        result = lax.all_to_all(result, axes[k], k, k, tiled=True)
    return result.reshape(-1, *inside)


def two_step_exchange(array, groups, turns, split_dim, concat_dim):
    size = lax.axis_size(groups[0]) * lax.axis_size(groups[1])
    pieces = split_up(array, split_dim, size)
    return in_order(turned_blocks(pieces, groups, turns), concat_dim)


def window_mask(box, start, rows, tile_w):
    row_ids = start[..., None, None] + jnp.arange(rows, dtype=jnp.int32)[:, None]
    col_ids = jnp.arange(tile_w, dtype=jnp.int32)[None, :]
    inside = (row_ids >= box[..., 0, None, None]) & (row_ids < box[..., 1, None, None])
    inside = inside & (col_ids >= box[..., 2, None, None]) & (col_ids < box[..., 3, None, None])
    return inside.reshape(box.shape[:-1] + (rows * tile_w,))


def fetch_limit(nearest):
    band_limit = gathered_copies(nearest[None, :], "wide", 0)
    return band_limit


def per_device(
    surf_depth, surf_color, surf_box, vol_color, vol_alpha, vol_box, ray_entry, ray_step, order
):
    tile_pix = TILE_H * TILE_W
    depth = surf_depth[0, 0]
    color = surf_color[0, 0]
    sbox = surf_box[0, 0]
    s_inside = window_mask(sbox, jnp.zeros_like(sbox[:, 0]), TILE_H, TILE_W)
    send_depth = jnp.where(s_inside, depth, far_depth)
    send_color = jnp.where(s_inside[:, None, :], color, jnp.zeros((), jnp.bfloat16))
    frag_depth = two_step_exchange(send_depth, ("grp_0", "grp_1"), (1, 0), 0, 0)
    frag_color = two_step_exchange(send_color, ("grp_0", "grp_1"), (1, 0), 0, 0)
    nearest = jnp.min(frag_depth, axis=0)
    winner = jnp.argmin(frag_depth, axis=0)
    pick = (jnp.arange(frag_depth.shape[0], dtype=jnp.int32)[:, None] == winner[None, :]) & (
        frag_depth < far_depth
    )
    surface = jnp.sum(jnp.where(pick[:, None, :], frag_color.astype(jnp.float32), 0.0), axis=0)
    vcolor = vol_color[0, 0]
    valpha = vol_alpha[0, 0]
    vbox = vol_box[0, 0]
    entry = ray_entry[0, 0]
    stride = ray_step[0, 0]
    v_inside = window_mask(vbox, jnp.zeros_like(vbox[:, 0]), TILE_H, TILE_W)
    samples = valpha.shape[1]
    accum = jnp.zeros((valpha.shape[0], 3, valpha.shape[2]), jnp.float32)
    trans = jnp.ones((valpha.shape[0], valpha.shape[2]), jnp.float32)
    limit = fetch_limit(nearest)
    for k in range(samples):
        kept = v_inside & (entry + k * stride < limit)
        opacity = valpha[:, k].astype(jnp.float32)
        weight = jnp.where(kept, trans * opacity, 0.0)
        accum = accum + weight[:, None, :] * vcolor[:, k].astype(jnp.float32)
        trans = trans * (1.0 - jnp.where(kept, opacity, 0.0))
    layer_accum, layer_trans = (
        lax.all_to_all(accum, "wide", split_axis=0, concat_axis=0, tiled=True),
        lax.all_to_all(trans, "wide", split_axis=0, concat_axis=0, tiled=True),
    )
    rank = order[0]
    ordered_accum = jnp.take(layer_accum, rank, axis=0)
    ordered_trans = jnp.take(layer_trans, rank, axis=0)

    def over(carry, layer):
        color_sum, through = carry
        return ((color_sum + through[None, :] * layer[0], through * layer[1]), None)

    start = (jnp.zeros((3, tile_pix), jnp.float32), jnp.ones((tile_pix,), jnp.float32))
    (color_sum, through), unused = lax.scan(over, start, (ordered_accum, ordered_trans))
    rgb = color_sum + through[None, :] * surface
    frame = jnp.concatenate([rgb, through[None, :]], axis=0)
    return frame[None, None]


def solution(mesh):
    finer = Mesh(mesh.devices.reshape(mesh.shape["wide"], 8, 2), ("wide", "grp_0", "grp_1"))
    return jax.shard_map(
        per_device,
        mesh=finer,
        in_specs=(
            P("wide", GRP, None, None),
            P("wide", GRP, None, None, None),
            P("wide", GRP, None, None),
            P("wide", GRP, None, None, None, None),
            P("wide", GRP, None, None, None),
            P("wide", GRP, None, None),
            P("wide", GRP, None, None),
            P("wide", GRP, None, None),
            P(GRP, None),
        ),
        out_specs=P(GRP, "wide", None, None),
        check_vma=False,
    )
```

profile of v0, /device:TPU:8, one launch (start us, length us, event | category | flops | bytes accessed | tf_op | source)
XLA Modules:
  0.0 110.0 jit_solution(14294371552709939799)
XLA Ops:
  3.7 3.4 %all-to-all-start = ((s32[8,2,1,4096]{3,0,2,1:T(8,128)}), s32[8,2,1,4096]{3,0,2,1:T(8,128)S(1)}, u32[]{:S(2)}, u32[]{:S(2)}) async-start(s32[8,2,1,4096]{3,0,2,1:T(8,128)} %copy.68), calls=%async_computation | async-start | bytes 524288 | tf_op jit(solution)/shard_map/all_to_all | solution.py:40
  10.3 3.5 %all-to-all-start.5 = ((bf16[8,2,1,3,4096]{4,0,3,2,1:T(8,128)(2,1)}), bf16[8,2,1,3,4096]{4,0,3,2,1:T(8,128)(2,1)S(1)}, u32[]{:S(2)}, u32[]{:S(2)}) async-start(bf16[8,2,1,3,4096]{4,0,3,2,1:T(8,128)(2,1)} %copy.83), calls=%async_computation.5 | async-start | bytes 786432 | tf_op jit(solution)/shard_map/all_to_all | solution.py:40
  15.4 8.5 %all-to-all-start.1 = ((s32[8,2,1,4096]{3,1,2,0:T(2,128)}), s32[8,2,1,4096]{3,1,2,0:T(2,128)S(1)}, u32[]{:S(2)}, u32[]{:S(2)}) async-start(s32[8,2,1,4096]{3,1,2,0:T(2,128)} %copy.69), calls=%async_computation.1 | async-start | bytes 524288 | tf_op jit(solution)/shard_map/all_to_all | solution.py:40
  24.7 1.6 %copy.106 = bf16[1,1,16,8,4096]{4,2,3,1,0:T(8,128)(2,1)} copy(bf16[1,1,16,8,4096]{4,3,2,1,0:T(8,128)(2,1)S(1)} %copy-done.2) | data formatting | bytes 2097152 | tf_op args[4]
  26.3 3.7 %copy.105 = bf16[1,1,16,8,3,4096]{5,2,4,3,1,0:T(8,128)(2,1)S(1)} copy(bf16[1,1,16,8,3,4096]{5,3,4,2,1,0:T(8,128)(2,1)} %param.14) | data formatting | bytes 6291456 | tf_op args[3]
  29.9 1.2 %copy.84 = bf16[8,2,1,3,4096]{4,1,3,2,0:T(2,128)(2,1)} copy(bf16[8,2,1,3,4096]{4,0,3,2,1:T(8,128)(2,1)S(1)} %copy-done.1) | data formatting | bytes 786432 | tf_op jit(solution)/shard_map/all_to_all | solution.py:40
  32.8 3.3 %all-to-all-done.1 = s32[8,2,1,4096]{3,1,2,0:T(2,128)S(1)} async-done(((s32[8,2,1,4096]{3,1,2,0:T(2,128)}), s32[8,2,1,4096]{3,1,2,0:T(2,128)S(1)}, u32[]{:S(2)}, u32[]{:S(2)}) %all-to-all-start.1) | async-done | bytes 262176 | tf_op jit(solution)/shard_map/all_to_all | solution.py:40
  36.1 4.1 %all-to-all-start.6 = ((bf16[8,2,1,3,4096]{4,1,3,2,0:T(2,128)(2,1)}), bf16[8,2,1,3,4096]{4,1,3,2,0:T(2,128)(2,1)}, u32[]{:S(2)}, u32[]{:S(2)}) async-start(bf16[8,2,1,3,4096]{4,1,3,2,0:T(2,128)(2,1)} %copy.84), calls=%async_computation.6 | async-start | bytes 786432 | tf_op jit(solution)/shard_map/all_to_all | solution.py:40
  41.8 1.7 %iota_reduce_fusion = (s32[4096]{0:T(1024)}, s32[4096]{0:T(1024)}) fusion(s32[16,4096]{1,0:T(8,128)} %reshape_reshape.2), kind=kLoop, calls=%fused_computation.101 | loop fusion | flops 430080 | bytes 294912 | tf_op jit(solution)/shard_map/per_device/reduce | solution.py:76
  43.5 11.0 %all-to-all-done.6 = bf16[8,2,1,3,4096]{4,1,3,2,0:T(2,128)(2,1)} async-done(((bf16[8,2,1,3,4096]{4,1,3,2,0:T(2,128)(2,1)}), bf16[8,2,1,3,4096]{4,1,3,2,0:T(2,128)(2,1)}, u32[]{:S(2)}, u32[]{:S(2)}) %all-to-all-start.6) | async-done | bytes 393248 | tf_op jit(solution)/shard_map/all_to_all | solution.py:40
  54.6 1.6 %broadcast_in_dim.100 = s32[16,1,4096]{2,1,0:T(1,128)} broadcast(s32[4096]{0:T(1024)} %reduce_min.9), dimensions={2} | broadcast | bytes 278528 | tf_op jit(solution)/shard_map/broadcast_in_dim | solution.py:16
  56.2 7.4 %all-to-all-start.2 = ((s32[16,1,4096]{2,1,0:T(1,128)}), s32[16,1,4096]{2,1,0:T(1,128)}, u32[]{:S(2)}, u32[]{:S(2)}) async-start(s32[16,1,4096]{2,1,0:T(1,128)} %broadcast_in_dim.100), calls=%async_computation.2 | async-start | bytes 524288 | tf_op jit(solution)/shard_map/all_to_all | solution.py:17
  64.6 2.2 %select_reduce_fusion = f32[3,4096]{1,0:T(4,128)} fusion(bf16[8,2,1,3,4096]{4,1,3,2,0:T(2,128)(2,1)} %all-to-all-done.6, pred[8,2,4096]{2,1,0:T(4,128)(4,1)S(1)} %bitcast_and_fusion), kind=kLoop, calls=%fused_computation.23 | loop fusion | flops 577536 | bytes 507904 | tf_op jit(solution)/shard_map/reduce_sum | solution.py:80
  66.8 3.9 %all-to-all-done.2 = s32[16,1,4096]{2,1,0:T(1,128)} async-done(((s32[16,1,4096]{2,1,0:T(1,128)}), s32[16,1,4096]{2,1,0:T(1,128)}, u32[]{:S(2)}, u32[]{:S(2)}) %all-to-all-start.2) | async-done | bytes 262176 | tf_op jit(solution)/shard_map/all_to_all | solution.py:17
  70.7 3.3 %fusion.35 = (f32[16,1,4096]{2,0,1:T(8,128)S(1)}, pred[16,1,4096]{2,0,1:T(8,128)(4,1)}, f32[16,1,4096]{2,0,1:T(8,128)S(1)}, pred[16,1,4096]{2,0,1:T(8,128)(4,1)}...) fusion(bf16[16,8,4096]{2,0,1:T(8,128)(2,1)} %bitcast.203, ...), kind=kLoop, calls=%fused_computation.78 | loop fusion | flops 3932160 | bytes 3211264 | tf_op jit(solution)/shard_map/mul | solution.py:96
  74.9 5.5 %all-to-all-start.4 = ((f32[16,1,4096]{2,1,0:T(1,128)}), f32[16,1,4096]{2,1,0:T(1,128)}, u32[]{:S(2)}, u32[]{:S(2)}) async-start(f32[16,1,4096]{2,1,0:T(1,128)} %copy.81), calls=%async_computation.4 | async-start | bytes 524288 | tf_op jit(solution)/shard_map/all_to_all | solution.py:99
  80.4 1.4 %fusion.21 = (f32[16,4096]{1,0:T(8,128)S(1)}, f32[16,4096]{1,0:T(8,128)S(1)}, f32[16,4096]{1,0:T(8,128)S(1)}) fusion(pred[16,1,4096]{2,0,1:T(8,128)(4,1)} %get-tuple-element.80, bf16[16,8,4096]{2,0,1:T(8,128)(2,1)} %bitcast.204, f32[16,1,4096]{2,0,1:T(8,128)} %get-tuple-element.76, pred[16,1,4096]{2,0,1:T(8,128)(4,1)} %get-tuple-element.75, ...), kind=kLoop, calls=%fused_computation.64 | loop fusion | flops 983040 | bytes 1638400 | tf_op jit(solution)/shard_map/mul | solution.py:95
  81.8 1.5 %fusion.9 = (f32[16,4096]{1,0:T(8,128)S(1)}, f32[16,4096]{1,0:T(8,128)S(1)}, f32[16,4096]{1,0:T(8,128)S(1)}, f32[16,4096]{1,0:T(8,128)S(1)}, f32[16,4096]{1,0:T(8,128)S(1)}) fusion(pred[16,1,4096]{2,0,1:T(8,128)(4,1)} %get-tuple-element.78, pred[16,1,4096]{2,0,1:T(8,128)(4,1)} %get-tuple-element.77, bf16[16,8,4096]{2,0,1:T(8,128)(2,1)} %bitcast.205, ...), kind=kLoop, calls=%fused_computation.52 | loop fusion | flops 1376256 | bytes 2555904 | tf_op jit(solution)/shard_map/mul | solution.py:95
  84.0 1.5 %copy.80 = f32[16,3,4096]{2,1,0:T(4,128)} copy(f32[16,3,4096]{2,0,1:T(8,128)S(1)} %fusion.1) | data formatting | bytes 1572864 | tf_op jit(solution)/shard_map/add | solution.py:95
  85.5 2.0 %all-to-all-done.4 = f32[16,1,4096]{2,1,0:T(1,128)} async-done(((f32[16,1,4096]{2,1,0:T(1,128)}), f32[16,1,4096]{2,1,0:T(1,128)}, u32[]{:S(2)}, u32[]{:S(2)}) %all-to-all-start.4) | async-done | bytes 262176 | tf_op jit(solution)/shard_map/all_to_all | solution.py:99
  87.6 5.2 %all-to-all-start.3 = ((f32[16,3,4096]{2,1,0:T(4,128)}), f32[16,3,4096]{2,1,0:T(4,128)S(1)}, u32[]{:S(2)}, u32[]{:S(2)}) async-start(f32[16,3,4096]{2,1,0:T(4,128)} %copy.80), calls=%async_computation.3 | async-start | bytes 2097152 | tf_op jit(solution)/shard_map/all_to_all | solution.py:98
  94.8 10.7 %all-to-all-done.3 = f32[16,3,4096]{2,1,0:T(4,128)S(1)} async-done(((f32[16,3,4096]{2,1,0:T(4,128)}), f32[16,3,4096]{2,1,0:T(4,128)S(1)}, u32[]{:S(2)}, u32[]{:S(2)}) %all-to-all-start.3) | async-done | bytes 786464 | tf_op jit(solution)/shard_map/all_to_all | solution.py:98
  105.5 1.3 %gather_fusion = f32[16,3,4096]{2,1,0:T(4,128)S(1)} fusion(f32[16,3,4096]{2,1,0:T(4,128)S(1)} %all-to-all-done.3, s32[1024]{0:T(1024)} %pad_clamp_fusion), kind=kCustom, calls=%fused_computation | custom fusion | bytes 1572928 | tf_op jit(solution)/shard_map/jit(_take)/gather | solution.py:102
  107.1 2.2 %while.13 = (s32[]{:T(128)}, f32[3,4096]{1,0:T(4,128)S(1)}, f32[4096]{0:T(1024)S(1)}, f32[16,3,4096]{2,1,0:T(4,128)S(1)}, f32[16,4096]{1,0:T(8,128)S(1)}, /*index=5*/s32[]{:T(128)}, s32[]{:T(128)}) while((s32[]{:T(128)}, f32[3,4096]{1,0:T(4,128)S(1)}, f32[4096]{0:T(1024)S(1)}, f32[16,3,4096]{2,1,0:T(4,128)S(1)}, ...), condition=%wide.region_2.3_spmd.clone, body=%wide.region_1.2_spmd.clone.sunk | while | flops 45059 | bytes 262248 | solution.py:110
  (103 shorter events, 19.8 us)
Async XLA Ops:
  0.0 8.2 %copy-start.3 = (bf16[1,1,16,3,4096]{4,2,3,1,0:T(8,128)(2,1)S(1)}, bf16[1,1,16,3,4096]{4,2,3,1,0:T(8,128)(2,1)}, u32[]{:S(2)}) copy-start(bf16[1,1,16,3,4096]{4,2,3,1,0:T(8,128)(2,1)} %param.12) | copy-start | bytes 1179652
  2.6 21.3 %copy-start.7 = (s32[1,16]{1,0:T(1,128)S(1)}, s32[1,16]{1,0:T(1,128)}, u32[]{:S(2)}) copy-start(s32[1,16]{1,0:T(1,128)} %param.19) | copy-start | bytes 196
  2.8 21.9 %copy-start.2 = (bf16[1,1,16,8,4096]{4,3,2,1,0:T(8,128)(2,1)S(1)}, bf16[1,1,16,8,4096]{4,3,2,1,0:T(8,128)(2,1)}, u32[]{:S(2)}) copy-start(bf16[1,1,16,8,4096]{4,3,2,1,0:T(8,128)(2,1)} %param.15) | copy-start | bytes 3145732
  3.7 6.6 %all-to-all-start = ((s32[8,2,1,4096]{3,0,2,1:T(8,128)}), s32[8,2,1,4096]{3,0,2,1:T(8,128)S(1)}, u32[]{:S(2)}, u32[]{:S(2)}) async-start(s32[8,2,1,4096]{3,0,2,1:T(8,128)} %copy.68), calls=%async_computation | async-start | bytes 524288 | tf_op jit(solution)/shard_map/all_to_all | solution.py:40
  10.3 5.1 %all-to-all-start.5 = ((bf16[8,2,1,3,4096]{4,0,3,2,1:T(8,128)(2,1)}), bf16[8,2,1,3,4096]{4,0,3,2,1:T(8,128)(2,1)S(1)}, u32[]{:S(2)}, u32[]{:S(2)}) async-start(bf16[8,2,1,3,4096]{4,0,3,2,1:T(8,128)(2,1)} %copy.83), calls=%async_computation.5 | async-start | bytes 786432 | tf_op jit(solution)/shard_map/all_to_all | solution.py:40
  15.4 9.2 %copy-start = (bf16[8,2,1,3,4096]{4,0,3,2,1:T(8,128)(2,1)}, bf16[8,2,1,3,4096]{4,0,3,2,1:T(8,128)(2,1)S(1)}, u32[]{:S(2)}) copy-start(bf16[8,2,1,3,4096]{4,0,3,2,1:T(8,128)(2,1)S(1)} %all-to-all-done.5) | copy-start | bytes 1179652
  15.4 20.6 %all-to-all-start.1 = ((s32[8,2,1,4096]{3,1,2,0:T(2,128)}), s32[8,2,1,4096]{3,1,2,0:T(2,128)S(1)}, u32[]{:S(2)}, u32[]{:S(2)}) async-start(s32[8,2,1,4096]{3,1,2,0:T(2,128)} %copy.69), calls=%async_computation.1 | async-start | bytes 524288 | tf_op jit(solution)/shard_map/all_to_all | solution.py:40
  26.3 3.7 %copy-start.1 = (bf16[8,2,1,3,4096]{4,0,3,2,1:T(8,128)(2,1)S(1)}, bf16[8,2,1,3,4096]{4,0,3,2,1:T(8,128)(2,1)}, u32[]{:S(2)}) copy-start(bf16[8,2,1,3,4096]{4,0,3,2,1:T(8,128)(2,1)} %copy-done) | copy-start | bytes 1179652
  26.3 5.5 %copy-start.6 = (s32[16]{0:T(128)S(1)}, s32[16]{0:T(128)}, u32[]{:S(2)}) copy-start(s32[16]{0:T(128)} %fusion.61) | copy-start | bytes 196
  26.3 6.1 %copy-start.8 = (s32[1,16]{1,0:T(1,128)S(1)}, s32[1,16]{1,0:T(1,128)}, u32[]{:S(2)}) copy-start(s32[1,16]{1,0:T(1,128)} %param.19) | copy-start | bytes 196
  36.1 18.5 %all-to-all-start.6 = ((bf16[8,2,1,3,4096]{4,1,3,2,0:T(2,128)(2,1)}), bf16[8,2,1,3,4096]{4,1,3,2,0:T(2,128)(2,1)}, u32[]{:S(2)}, u32[]{:S(2)}) async-start(bf16[8,2,1,3,4096]{4,1,3,2,0:T(2,128)(2,1)} %copy.84), calls=%async_computation.6 | async-start | bytes 786432 | tf_op jit(solution)/shard_map/all_to_all | solution.py:40
  56.2 14.5 %all-to-all-start.2 = ((s32[16,1,4096]{2,1,0:T(1,128)}), s32[16,1,4096]{2,1,0:T(1,128)}, u32[]{:S(2)}, u32[]{:S(2)}) async-start(s32[16,1,4096]{2,1,0:T(1,128)} %broadcast_in_dim.100), calls=%async_computation.2 | async-start | bytes 524288 | tf_op jit(solution)/shard_map/all_to_all | solution.py:17
  74.9 12.7 %all-to-all-start.4 = ((f32[16,1,4096]{2,1,0:T(1,128)}), f32[16,1,4096]{2,1,0:T(1,128)}, u32[]{:S(2)}, u32[]{:S(2)}) async-start(f32[16,1,4096]{2,1,0:T(1,128)} %copy.81), calls=%async_computation.4 | async-start | bytes 524288 | tf_op jit(solution)/shard_map/all_to_all | solution.py:99
  84.0 10.7 %copy-start.5 = (pred[16]{0:T(512)(128)(4,1)S(1)}, pred[16]{0:T(512)(128)(4,1)}, u32[]{:S(2)}) copy-start(pred[16]{0:T(512)(128)(4,1)} %compare_and_fusion) | copy-start | bytes 52
  87.6 17.9 %all-to-all-start.3 = ((f32[16,3,4096]{2,1,0:T(4,128)}), f32[16,3,4096]{2,1,0:T(4,128)S(1)}, u32[]{:S(2)}, u32[]{:S(2)}) async-start(f32[16,3,4096]{2,1,0:T(4,128)} %copy.80), calls=%async_computation.3 | async-start | bytes 2097152 | tf_op jit(solution)/shard_map/all_to_all | solution.py:98
  94.7 14.6 %copy-start.4 = (f32[3,4096]{1,0:T(4,128)S(1)}, f32[3,4096]{1,0:T(4,128)}, u32[]{:S(2)}) copy-start(f32[3,4096]{1,0:T(4,128)} %select_reduce_fusion) | copy-start | bytes 147460
where the time goes:
time: 111 us; the launch traced here: 110 us
  starting transfers between devices  37.6 us (34%)
  waiting for transfers between devices  31.7 us (29%)
  local copies, waits for them, and re-layouts  21.5 us (19%)
  other arithmetic  18.6 us (17%)
    all_to_all x4, starting transfers between devices, turned_blocks(): result = lax.all_to_all(result, axes[k], k, k, tiled=True)  19.5 us
    all_to_all x4, waiting for transfers between devices, turned_blocks(): result = lax.all_to_all(result, axes[k], k, k, tiled=True)  15 us
    all_to_all x1, waiting for transfers between devices, per_device(): lax.all_to_all(accum, 'wide', split_axis=0, concat_axis=0, tiled=True)  10.7 us
    all_to_all x1, starting transfers between devices, sent_to_all(): return lax.all_to_all(copies, axis, split_axis=0, concat_axis=0, tiled=True)  7.39 us
    unnamed x21, local copies, waits for them, and re-layouts  6.39 us
    all_to_all x1, starting transfers between devices, per_device(): lax.all_to_all(trans, 'wide', split_axis=0, concat_axis=0, tiled=True)  5.51 us
    all_to_all x1, starting transfers between devices, per_device(): lax.all_to_all(accum, 'wide', split_axis=0, concat_axis=0, tiled=True)  5.24 us
    all_to_all x1, waiting for transfers between devices, sent_to_all(): return lax.all_to_all(copies, axis, split_axis=0, concat_axis=0, tiled=True)  3.9 us
  transfers between devices with their start and end apart: 7, of which 6 were waited for; matrix products, arithmetic and copies ran while one was open for 24% of the time, Pallas kernels for 0%

commit v1 on v0

v1 whole, which is shorter than its diff:
```python
import functools

import jax
import jax.numpy as jnp
from jax import lax
from jax.experimental import pallas as pl
from jax.experimental.pallas import tpu as pltpu
from jax.sharding import PartitionSpec as P

MESH = pl.DeviceIdType.MESH
FAR = 1073741824
PIX = 4096
LROWS = 32
S = 40
SAMPLES = 8
COLOR_SCALE = 59000.0
ALPHA_SCALE = 236000.0

I32 = jnp.int32
F32 = jnp.float32


def far_first(nx, ny):
    ring = lambda d, n: min(d, n - d)
    offsets = [(a, b) for a in range(nx) for b in range(ny) if (a, b) != (0, 0)]
    return sorted(offsets, key=lambda o: -(ring(o[0], nx) + ring(o[1], ny)))


def kernel(
    dims,
    sdepth, scolor, sbox, vcolor, valpha, vbox, entry, step, order,
    out,
    sd_nat, sc_nat, vc_nat, va_nat, en_nat, st_nat,
    sd, sc, en, st, ad, cd,
    a_send, a_recv, c_send, c_recv, t_send, t_recv, l_send, l_recv, f_send, f_recv,
    tab0, tab1, surf, od,
    lsem, a_ss, a_rs, c_ss, c_rs, t_ss, t_rs, l_ss, l_rs, f_ss, f_rs,
):
    nx, ny, nz, ncore = dims
    nw, ng = nx * ny, nz * ncore
    me_w, me_g = lax.axis_index("wide"), lax.axis_index("grp")
    wide_offsets, grp_offsets = far_first(nx, ny), far_first(nz, ncore)

    def wide_peer(o):
        x, y = me_w // ny, me_w % ny
        return ((x + o[0]) % nx) * ny + (y + o[1]) % ny

    def grp_peer(o):
        z, core = me_g // ncore, me_g % ncore
        return ((z + o[0]) % nz) * ncore + (core + o[1]) % ncore

    def wide_copy(o, src, dst, ss, rs):
        peer = wide_peer(o)
        return pltpu.make_async_remote_copy(
            src_ref=src.at[peer], dst_ref=dst.at[me_w], send_sem=ss.at[peer], recv_sem=rs.at[me_w],
            device_id=(peer, me_g), device_id_type=MESH,
        )

    def grp_copy(o, src, dst, ss, rs):
        peer = grp_peer(o)
        return pltpu.make_async_remote_copy(
            src_ref=src.at[peer], dst_ref=dst.at[me_g], send_sem=ss.at[peer], recv_sem=rs.at[me_g],
            device_id=(me_w, peer), device_id_type=MESH,
        )

    def arrived(peer, buf, rs):
        pltpu.make_async_copy(buf.at[peer], buf.at[peer], rs.at[peer]).wait()

    def left(peer, buf, ss):
        pltpu.make_async_copy(buf.at[peer], buf.at[peer], ss.at[peer]).wait()

    loads = []
    for i, (src, dst) in enumerate(
        ((sdepth, sd_nat), (valpha, va_nat), (vcolor, vc_nat), (entry, en_nat), (step, st_nat), (scolor, sc_nat))
    ):
        loads.append(pltpu.make_async_copy(src, dst, lsem.at[i]))
        loads[-1].start()

    barrier = pltpu.get_barrier_semaphore()
    for o in grp_offsets:
        pl.semaphore_signal(barrier, inc=1, device_id=(me_w, grp_peer(o)), device_id_type=MESH)
    for o in wide_offsets:
        pl.semaphore_signal(barrier, inc=1, device_id=(wide_peer(o), me_g), device_id_type=MESH)

    row8 = lax.broadcasted_iota(I32, (8, 128), 0)
    lane8 = lax.broadcasted_iota(I32, (8, 128), 1)
    fold8 = 2 * row8 + (lane8 >> 6)
    col8 = lane8 & 63
    fold16 = 2 * lax.broadcasted_iota(I32, (16, 128), 0) + (lax.broadcasted_iota(I32, (16, 128), 1) >> 6)
    col16 = lax.broadcasted_iota(I32, (16, 128), 1) & 63

    def spread(nat, dense, n, lead=()):
        g = min(8, n)
        for h in range(n // g):
            for j in range(LROWS):
                tile = nat[(*lead, pl.ds(h * g, g), pl.ds(128 * j, 128))]
                if tile.dtype == jnp.bfloat16:
                    tile = tile.astype(F32)
                dense[pl.ds(h * g * S + j, g, stride=S), :] = tile

    loads[0].wait()
    spread(sd_nat, sd, ng)

    def surface_inside(r):
        inx = (col8 >= sbox[2, r]) & (col8 < sbox[3, r])
        return [
            inx & (fold8 + 16 * q >= sbox[0, r]) & (fold8 + 16 * q < sbox[1, r]) for q in range(4)
        ]

    for r in range(ng):
        folded = jnp.full((8, 128), FAR, I32)
        for q, inside in enumerate(surface_inside(r)):
            folded = jnp.where(inside, sd[pl.ds(r * S + 8 * q, 8), :], folded)
        a_send[r, 0:8, :] = folded
        a_send[r, 8:9, :] = jnp.full((1, 128), sbox[0, r], I32)
    for c in range(nw):
        t_send[c] = jnp.full((1, 128), vbox[0, c], I32)
    a_recv[me_g] = a_send[me_g]
    t_recv[me_w] = t_send[me_w]

    pl.semaphore_wait(barrier, nw + ng - 2)
    for o in grp_offsets:
        grp_copy(o, a_send, a_recv, a_ss, a_rs).start()
    for o in wide_offsets:
        wide_copy(o, t_send, t_recv, t_ss, t_rs).start()

    loads[5].wait()
    for ch in range(3):
        spread(sc_nat, sc.at[ch], ng, (ch,))

    def fold_color(r, carry):
        inside = surface_inside(r)
        for ch in range(3):
            folded = jnp.zeros((8, 128), F32)
            for q in range(4):
                folded = jnp.where(inside[q], sc[ch, pl.ds(r * S + 8 * q, 8), :], folded)
            c_send[r, ch] = folded.astype(jnp.bfloat16)
        return carry

    lax.fori_loop(0, ng, fold_color, 0)
    c_recv[me_g] = c_send[me_g]

    for i in (1, 2, 3, 4):
        loads[i].wait()
    spread(en_nat, en, nw)
    spread(st_nat, st, nw)

    lane1 = lax.broadcasted_iota(I32, (8, 128), 1) >> 6

    def prefixes(c, carry):
        top, bottom = vbox[0, c], vbox[1, c]
        for j in range(16):
            s = lane1 + 2 * j
            upper = (top + ((s - top) & 31)) >= 32
            px, px2 = pl.ds(128 * j, 128), pl.ds(128 * (j + 16), 128)
            ad[pl.ds(j, SAMPLES, stride=S), :] = jnp.where(
                upper, va_nat[c, :, px2].astype(F32), va_nat[c, :, px].astype(F32)
            )
            for ch in range(3):
                cd[ch, pl.ds(j, SAMPLES, stride=S), :] = jnp.where(
                    upper, vc_nat[c, ch, :, px2].astype(F32), vc_nat[c, ch, :, px].astype(F32)
                )
        y = top + ((fold16 - top) & 31)
        upper = y >= 32
        inside = (y < bottom) & (col16 >= vbox[2, c]) & (col16 < vbox[3, c])
        first = jnp.where(upper, en[pl.ds(c * S + 16, 16), :], en[pl.ds(c * S, 16), :])
        en[pl.ds(c * S, 16), :] = jnp.where(inside, first, FAR)
        st[pl.ds(c * S, 16), :] = jnp.where(upper, st[pl.ds(c * S + 16, 16), :], st[pl.ds(c * S, 16), :])
        trans = jnp.ones((16, 128), F32)
        accum = [jnp.zeros((16, 128), F32) for _ in range(3)]
        for k in range(SAMPLES):
            alpha = ad[pl.ds(k * S, 16), :]
            weight = trans * alpha
            trans = trans * (1.0 - alpha)
            for ch in range(3):
                accum[ch] = accum[ch] + weight * cd[ch, pl.ds(k * S, 16), :]
            r, g, b = [(a * COLOR_SCALE + 0.5).astype(I32) for a in accum]
            t = ((1.0 - trans) * ALPHA_SCALE + 0.5).astype(I32)
            tab0[c, k] = (r << 16) | g
            tab1[c, k] = (b << 16) | t
        return carry

    lax.fori_loop(0, nw // 2, prefixes, 0)

    for o in reversed(grp_offsets):
        arrived(grp_peer(o), a_recv, a_rs)
    near = [jnp.full((8, 128), FAR, I32) for _ in range(4)]
    winner = [jnp.full((8, 128), -1, I32) for _ in range(4)]
    for s in range(ng):
        depth = a_recv[s, 0:8, :]
        top = a_recv[s, 8:9, :]
        where_q = (top + ((fold8 - top) & 15)) >> 4
        for q in range(4):
            take = (where_q == q) & (depth < near[q])
            near[q] = jnp.where(take, depth, near[q])
            winner[q] = jnp.where(take, s, winner[q])

    for o in reversed(wide_offsets):
        arrived(wide_peer(o), t_recv, t_rs)

    def upper_half(top):
        return (top + ((fold16 - top) & 31)) >= 32

    near_lo = jnp.concatenate(near[:2], axis=0)
    near_hi = jnp.concatenate(near[2:], axis=0)
    for b in range(nw):
        l_send[b] = jnp.where(upper_half(t_recv[b]), near_hi, near_lo)
    l_recv[me_w] = l_send[me_w]
    for o in wide_offsets:
        wide_copy(o, l_send, l_recv, l_ss, l_rs).start()
    for o in grp_offsets:
        grp_copy(o, c_send, c_recv, c_ss, c_rs).start()

    lax.fori_loop(nw // 2, nw, prefixes, 0)

    waiting = None
    for o in [(0, 0), *reversed(wide_offsets)]:
        c = wide_peer(o)
        if o != (0, 0):
            arrived(c, l_recv, l_rs)
        limit = l_recv[c]
        at = en[pl.ds(c * S, 16), :]
        stride = st[pl.ds(c * S, 16), :]
        word0 = jnp.zeros((16, 128), I32)
        word1 = jnp.zeros((16, 128), I32)
        for k in range(SAMPLES):
            kept = at < limit
            word0 = jnp.where(kept, tab0[c, k], word0)
            word1 = jnp.where(kept, tab1[c, k], word1)
            at = at + stride
        if o == (0, 0):
            f_recv[me_w, 0:16, :] = word0
            f_recv[me_w, 16:32, :] = word1
        else:
            f_send[c, 0:16, :] = word0
            f_send[c, 16:32, :] = word1
            if waiting is not None:
                wide_copy(waiting, f_send, f_recv, f_ss, f_rs).start()
            waiting = o
    for o in reversed(grp_offsets):
        arrived(grp_peer(o), c_recv, c_rs)
    wide_copy(waiting, f_send, f_recv, f_ss, f_rs).start()
    color = [[jnp.zeros((8, 128), F32) for _ in range(3)] for _ in range(4)]
    for s in range(ng):
        rgb = [c_recv[s, ch].astype(F32) for ch in range(3)]
        for q in range(4):
            won = winner[q] == s
            color[q] = [jnp.where(won, rgb[ch], color[q][ch]) for ch in range(3)]
    for ch in range(3):
        for q in range(4):
            surf[ch, 8 * q : 8 * q + 8, :] = color[q][ch]

    for o in reversed(wide_offsets):
        arrived(wide_peer(o), f_recv, f_rs)
    through = [jnp.ones((16, 128), F32) for _ in range(2)]
    total = [[jnp.zeros((16, 128), F32) for _ in range(3)] for _ in range(2)]
    for j in range(nw):
        b = order[0, j]
        word0, word1 = f_recv[b, 0:16, :], f_recv[b, 16:32, :]
        upper = upper_half(t_recv[b])
        layer = [
            lax.shift_right_logical(word0, 16).astype(F32),
            (word0 & 65535).astype(F32),
            lax.shift_right_logical(word1, 16).astype(F32),
        ]
        opaque = (word1 & 65535).astype(F32) * (1.0 / ALPHA_SCALE)
        for h in range(2):
            weight = jnp.where(upper, through[h], 0.0) if h else jnp.where(upper, 0.0, through[h])
            total[h] = [total[h][ch] + weight * layer[ch] for ch in range(3)]
            through[h] = through[h] - weight * opaque
    for h in range(2):
        rows = slice(16 * h, 16 * h + 16)
        for ch in range(3):
            od[ch * S + 16 * h : ch * S + 16 * h + 16, :] = (
                total[h][ch] * (1.0 / COLOR_SCALE) + through[h] * surf[ch, rows, :]
            )
        od[3 * S + 16 * h : 3 * S + 16 * h + 16, :] = through[h]
    for j in range(LROWS):
        out[:, 128 * j : 128 * j + 128] = od[pl.ds(j, 4, stride=S), :]

    for o in grp_offsets:
        left(grp_peer(o), a_send, a_ss)
        left(grp_peer(o), c_send, c_ss)
    for o in wide_offsets:
        left(wide_peer(o), t_send, t_ss)
        left(wide_peer(o), l_send, l_ss)
        left(wide_peer(o), f_send, f_ss)


def per_device(dims, surf_depth, surf_color, surf_box, vol_color, vol_alpha, vol_box, ray_entry, ray_step, order):
    nx, ny, nz, ncore = dims
    nw, ng = nx * ny, nz * ncore
    V, D = pltpu.VMEM, pltpu.SemaphoreType.DMA
    bf16 = jnp.bfloat16
    hbm = pl.BlockSpec(memory_space=pltpu.HBM)
    smem = pl.BlockSpec(memory_space=pltpu.SMEM)
    frame = pl.pallas_call(
        functools.partial(kernel, dims),
        out_shape=jax.ShapeDtypeStruct((4, PIX), F32),
        in_specs=[hbm, hbm, smem, hbm, hbm, smem, hbm, hbm, smem],
        out_specs=pl.BlockSpec(memory_space=pltpu.VMEM),
        scratch_shapes=[
            V((ng, PIX), I32), V((3, ng, PIX), bf16), V((nw, 3, SAMPLES, PIX), bf16), V((nw, SAMPLES, PIX), bf16),
            V((nw, PIX), I32), V((nw, PIX), I32),
            V((ng * S, 128), I32), V((3, ng * S, 128), F32), V((nw * S, 128), I32), V((nw * S, 128), I32),
            V((SAMPLES * S, 128), F32), V((3, SAMPLES * S, 128), F32),
            V((ng, 9, 128), I32), V((ng, 9, 128), I32),
            V((ng, 3, 8, 128), bf16), V((ng, 3, 8, 128), bf16),
            V((nw, 1, 128), I32), V((nw, 1, 128), I32),
            V((nw, 16, 128), I32), V((nw, 16, 128), I32),
            V((nw, 32, 128), I32), V((nw, 32, 128), I32),
            V((nw, SAMPLES, 16, 128), I32), V((nw, SAMPLES, 16, 128), I32),
            V((3, LROWS, 128), F32), V((4 * S, 128), F32),
            D((6,)), D((ng,)), D((ng,)), D((ng,)), D((ng,)), D((nw,)), D((nw,)), D((nw,)), D((nw,)), D((nw,)), D((nw,)),
        ],
        compiler_params=pltpu.CompilerParams(
            collective_id=0, has_side_effects=True, vmem_limit_bytes=67043328
        ),
    )(
        surf_depth[0, 0],
        jnp.transpose(surf_color[0, 0], (1, 0, 2)),
        surf_box[0, 0].T,
        jnp.transpose(vol_color[0, 0], (0, 2, 1, 3)),
        vol_alpha[0, 0],
        vol_box[0, 0].T,
        ray_entry[0, 0],
        ray_step[0, 0],
        order,
    )
    return frame[None, None]


def solution(mesh):
    nw, ng = mesh.shape["wide"], mesh.shape["grp"]
    nx = max(d for d in range(1, nw + 1) if d * d <= nw and nw % d == 0)
    dims = (nx, nw // nx, ng // 2, 2)
    return jax.shard_map(
        functools.partial(per_device, dims),
        mesh=mesh,
        in_specs=(
            P("wide", "grp", None, None),
            P("wide", "grp", None, None, None),
            P("wide", "grp", None, None),
            P("wide", "grp", None, None, None, None),
            P("wide", "grp", None, None, None),
            P("wide", "grp", None, None),
            P("wide", "grp", None, None),
            P("wide", "grp", None, None),
            P("grp", None),
        ),
        out_specs=P("grp", "wide", None, None),
        check_vma=False,
    )
```

time: 111 us -> 29.6 us (0.27)
  the two profiles are of different devices: /device:TPU:8 before, /device:TPU:1 now
where the time goes in v1:
time: 29.6 us; the launch traced here: 29.4 us
  Pallas kernels  27.9 us (94%)
  local copies, waits for them, and re-layouts  1.47 us (5%)
    pallas_call x1, Pallas kernels, per_device(): pl.pallas_call(functools.partial(kernel, dims), out_shape=jax.ShapeDtypeS...  27.9 us
    unnamed x1, local copies, waits for them, and re-layouts  1.47 us

profile of v1, /device:TPU:1, one launch (start us, length us, event | category | flops | bytes accessed | tf_op | source)
XLA Modules:
  0.0 29.4 jit_solution(14684510475900878273)
XLA Ops:
  0.0 27.9 %shard_map.91 = f32[4,4096]{1,0:T(4,128)} custom-call(s32[16,4096]{1,0:T(8,128)} %bitcast.21, bf16[3,16,4096]{2,1,0:T(8,128)(2,1)} %bitcast.19, s32[4,16]{1,0:T(4,128)} %bitcast.24, bf16[16,3,8,4096]{3,2,1,0:T(8,128)(2,1)} %bitcast.17, bf16[16,8,4096]{2,1,0:T(8,128)(2,1)} %bitcast.18, s32[4,16]{1,0:T(4,128)} %bitcast.25, s32[16,4096]{1,0:T(8,128)} %bitcast.22, ...), custom_call_target="tpu_custom_call" | custom-call | tf_op jit(solution)/shard_map/pallas_call | solution.py:297
  28.0 1.5 %copy.11 = f32[1,1,4,4096]{3,2,1,0:T(4,128)} copy(f32[1,1,4,4096]{3,2,1,0:T(4,128)} %bitcast.20) | data formatting | bytes 131072

commit v2 on v1

--- a/solution.py
+++ b/solution.py
@@ -28,13 +28,14 @@
 
 def kernel(
     dims,
-    sdepth, scolor, sbox, vcolor, valpha, vbox, entry, step, order,
+    sdepth, scolor, sbox_hbm, vcolor, valpha, vbox_hbm, entry, step, order_hbm,
     out,
+    sbox, vbox, order,
     sd_nat, sc_nat, vc_nat, va_nat, en_nat, st_nat,
     sd, sc, en, st, ad, cd,
     a_send, a_recv, c_send, c_recv, t_send, t_recv, l_send, l_recv, f_send, f_recv,
     tab0, tab1, surf, od,
-    lsem, a_ss, a_rs, c_ss, c_rs, t_ss, t_rs, l_ss, l_rs, f_ss, f_rs,
+    lsem, g_ready, w_ready, a_ss, a_rs, c_ss, c_rs, t_ss, t_rs, l_ss, l_rs, f_ss, f_rs,
 ):
     nx, ny, nz, ncore = dims
     nw, ng = nx * ny, nz * ncore
@@ -49,38 +50,58 @@
         z, core = me_g // ncore, me_g % ncore
         return ((z + o[0]) % nz) * ncore + (core + o[1]) % ncore
 
-    def wide_copy(o, src, dst, ss, rs):
-        peer = wide_peer(o)
+    def wide_copy(peer, src, dst, ss, rs):
         return pltpu.make_async_remote_copy(
-            src_ref=src.at[peer], dst_ref=dst.at[me_w], send_sem=ss.at[peer], recv_sem=rs.at[me_w],
+            src_ref=src.at[peer], dst_ref=dst.at[me_w], send_sem=ss, recv_sem=rs,
             device_id=(peer, me_g), device_id_type=MESH,
         )
 
-    def grp_copy(o, src, dst, ss, rs):
-        peer = grp_peer(o)
+    def grp_copy(peer, src, dst, ss, rs):
         return pltpu.make_async_remote_copy(
-            src_ref=src.at[peer], dst_ref=dst.at[me_g], send_sem=ss.at[peer], recv_sem=rs.at[me_g],
+            src_ref=src.at[peer], dst_ref=dst.at[me_g], send_sem=ss, recv_sem=rs,
             device_id=(me_w, peer), device_id_type=MESH,
         )
 
-    def arrived(peer, buf, rs):
-        pltpu.make_async_copy(buf.at[peer], buf.at[peer], rs.at[peer]).wait()
-
-    def left(peer, buf, ss):
-        pltpu.make_async_copy(buf.at[peer], buf.at[peer], ss.at[peer]).wait()
+    def all_of(n, buf, sem):
+        pltpu.make_async_copy(buf.at[pl.ds(0, n)], buf.at[pl.ds(0, n)], sem).wait()
+
+    half = ng // 2
+    barrier = pltpu.get_barrier_semaphore()
+
+    def greet(sem_g, sem_w, wants):
+        for o in grp_offsets:
+            peer = grp_peer(o)
+
+            @pl.when(wants(peer, me_g))
+            def _():
+                pl.semaphore_signal(sem_g, inc=1, device_id=(me_w, peer), device_id_type=MESH)
+
+        for o in wide_offsets:
+            peer = wide_peer(o)
+
+            @pl.when(wants(peer, me_w))
+            def _():
+                pl.semaphore_signal(sem_w, inc=1, device_id=(peer, me_g), device_id_type=MESH)
 
     loads = []
     for i, (src, dst) in enumerate(
-        ((sdepth, sd_nat), (valpha, va_nat), (vcolor, vc_nat), (entry, en_nat), (step, st_nat), (scolor, sc_nat))
+        (
+            (sbox_hbm, sbox), (sdepth, sd_nat), (vbox_hbm, vbox), (order_hbm, order), (scolor, sc_nat),
+            (valpha, va_nat), (vcolor, vc_nat), (entry, en_nat), (step, st_nat),
+        )
     ):
         loads.append(pltpu.make_async_copy(src, dst, lsem.at[i]))
-        loads[-1].start()
-
-    barrier = pltpu.get_barrier_semaphore()
-    for o in grp_offsets:
-        pl.semaphore_signal(barrier, inc=1, device_id=(me_w, grp_peer(o)), device_id_type=MESH)
-    for o in wide_offsets:
-        pl.semaphore_signal(barrier, inc=1, device_id=(wide_peer(o), me_g), device_id_type=MESH)
+        if i < 4:
+            loads[-1].start()
+    greet(barrier, barrier, lambda peer, me: peer > me)
+    for load in loads[4:]:
+        load.start()
+
+    def send_where(offsets, peer_of, me, copy, wants, *bufs):
+        for o in offsets:
+            pl.when(wants(peer_of(o), me))(lambda o=o: copy(peer_of(o), *bufs).start())
+
+    lower, higher = (lambda peer, me: peer < me), (lambda peer, me: peer > me)
 
     row8 = lax.broadcasted_iota(I32, (8, 128), 0)
     lane8 = lax.broadcasted_iota(I32, (8, 128), 1)
@@ -99,6 +120,7 @@
                 dense[pl.ds(h * g * S + j, g, stride=S), :] = tile
 
     loads[0].wait()
+    loads[1].wait()
     spread(sd_nat, sd, ng)
 
     def surface_inside(r):
@@ -113,18 +135,19 @@
             folded = jnp.where(inside, sd[pl.ds(r * S + 8 * q, 8), :], folded)
         a_send[r, 0:8, :] = folded
         a_send[r, 8:9, :] = jnp.full((1, 128), sbox[0, r], I32)
+    loads[2].wait()
     for c in range(nw):
         t_send[c] = jnp.full((1, 128), vbox[0, c], I32)
     a_recv[me_g] = a_send[me_g]
     t_recv[me_w] = t_send[me_w]
 
-    pl.semaphore_wait(barrier, nw + ng - 2)
-    for o in grp_offsets:
-        grp_copy(o, a_send, a_recv, a_ss, a_rs).start()
-    for o in wide_offsets:
-        wide_copy(o, t_send, t_recv, t_ss, t_rs).start()
-
-    loads[5].wait()
+    pl.when(me_g + me_w > 0)(lambda: pl.semaphore_wait(barrier, me_g + me_w))
+    greet(g_ready, w_ready, lambda peer, me: peer < me)
+
+    send_where(grp_offsets, grp_peer, me_g, grp_copy, lower, a_send, a_recv, a_ss, a_rs.at[me_g // half])
+    send_where(wide_offsets, wide_peer, me_w, wide_copy, lower, t_send, t_recv, t_ss, t_rs)
+
+    loads[4].wait()
     for ch in range(3):
         spread(sc_nat, sc.at[ch], ng, (ch,))
 
@@ -140,8 +163,8 @@
     lax.fori_loop(0, ng, fold_color, 0)
     c_recv[me_g] = c_send[me_g]
 
-    for i in (1, 2, 3, 4):
-        loads[i].wait()
+    for load in loads[5:]:
+        load.wait()
     spread(en_nat, en, nw)
     spread(st_nat, st, nw)
 
@@ -180,13 +203,20 @@
             tab1[c, k] = (b << 16) | t
         return carry
 
-    lax.fori_loop(0, nw // 2, prefixes, 0)
-
-    for o in reversed(grp_offsets):
-        arrived(grp_peer(o), a_recv, a_rs)
+    lax.fori_loop(0, nw, prefixes, 0)
+
+    pl.when(me_w < nw - 1)(lambda: pl.semaphore_wait(w_ready, nw - 1 - me_w))
+    send_where(wide_offsets, wide_peer, me_w, wide_copy, higher, t_send, t_recv, t_ss, t_rs)
+    pl.when(me_g < ng - 1)(lambda: pl.semaphore_wait(g_ready, ng - 1 - me_g))
+    send_where(grp_offsets, grp_peer, me_g, grp_copy, higher, a_send, a_recv, a_ss, a_rs.at[me_g // half])
+
     near = [jnp.full((8, 128), FAR, I32) for _ in range(4)]
     winner = [jnp.full((8, 128), -1, I32) for _ in range(4)]
     for s in range(ng):
+        if s % half == 0:
+            own = me_g // half == s // half
+            pl.when(own)(lambda: all_of(half - 1, a_recv, a_rs.at[s // half]))
+            pl.when(jnp.logical_not(own))(lambda: all_of(half, a_recv, a_rs.at[s // half]))
         depth = a_recv[s, 0:8, :]
         top = a_recv[s, 8:9, :]
         where_q = (top + ((fold8 - top) & 15)) >> 4
@@ -195,8 +225,7 @@
             near[q] = jnp.where(take, depth, near[q])
             winner[q] = jnp.where(take, s, winner[q])
 
-    for o in reversed(wide_offsets):
-        arrived(wide_peer(o), t_recv, t_rs)
+    all_of(nw - 1, t_recv, t_rs)
 
     def upper_half(top):
         return (top + ((fold16 - top) & 31)) >= 32
@@ -207,17 +236,19 @@
         l_send[b] = jnp.where(upper_half(t_recv[b]), near_hi, near_lo)
     l_recv[me_w] = l_send[me_w]
     for o in wide_offsets:
-        wide_copy(o, l_send, l_recv, l_ss, l_rs).start()
+        wide_copy(wide_peer(o), l_send, l_recv, l_ss, l_rs.at[me_w]).start()
     for o in grp_offsets:
-        grp_copy(o, c_send, c_recv, c_ss, c_rs).start()
-
-    lax.fori_loop(nw // 2, nw, prefixes, 0)
-
-    waiting = None
-    for o in [(0, 0), *reversed(wide_offsets)]:
-        c = wide_peer(o)
-        if o != (0, 0):
-            arrived(c, l_recv, l_rs)
+        grp_copy(grp_peer(o), c_send, c_recv, c_ss, c_rs).start()
+
+    def by_start():
+        for k in range(nx + ny - 1):
+            low, high = max(0, k - ny + 1), min(nx - 1, k)
+            for i in range(high - low + 1):
+                x = low + (me_w // ny + me_w % ny + i) % (high - low + 1)
+                yield x * ny + k - x
+
+    for c in by_start():
+        pl.when(me_w != c)(lambda c=c: pltpu.make_async_copy(l_recv.at[c], l_recv.at[c], l_rs.at[c]).wait())
         limit = l_recv[c]
         at = en[pl.ds(c * S, 16), :]
         stride = st[pl.ds(c * S, 16), :]
@@ -228,18 +259,15 @@
             word0 = jnp.where(kept, tab0[c, k], word0)
             word1 = jnp.where(kept, tab1[c, k], word1)
             at = at + stride
-        if o == (0, 0):
-            f_recv[me_w, 0:16, :] = word0
-            f_recv[me_w, 16:32, :] = word1
-        else:
-            f_send[c, 0:16, :] = word0
-            f_send[c, 16:32, :] = word1
-            if waiting is not None:
-                wide_copy(waiting, f_send, f_recv, f_ss, f_rs).start()
-            waiting = o
-    for o in reversed(grp_offsets):
-        arrived(grp_peer(o), c_recv, c_rs)
-    wide_copy(waiting, f_send, f_recv, f_ss, f_rs).start()
+        f_send[c, 0:16, :] = word0
+        f_send[c, 16:32, :] = word1
+
+        @pl.when(me_w != c)
+        def _(c=c):
+            wide_copy(c, f_send, f_recv, f_ss, f_rs).start()
+
+    f_recv[me_w] = f_send[me_w]
+    all_of(ng - 1, c_recv, c_rs)
     color = [[jnp.zeros((8, 128), F32) for _ in range(3)] for _ in range(4)]
     for s in range(ng):
         rgb = [c_recv[s, ch].astype(F32) for ch in range(3)]
@@ -250,10 +278,10 @@
         for q in range(4):
             surf[ch, 8 * q : 8 * q + 8, :] = color[q][ch]
 
-    for o in reversed(wide_offsets):
-        arrived(wide_peer(o), f_recv, f_rs)
+    all_of(nw - 1, f_recv, f_rs)
     through = [jnp.ones((16, 128), F32) for _ in range(2)]
     total = [[jnp.zeros((16, 128), F32) for _ in range(3)] for _ in range(2)]
+    loads[3].wait()
     for j in range(nw):
         b = order[0, j]
         word0, word1 = f_recv[b, 0:16, :], f_recv[b, 16:32, :]
@@ -278,13 +306,10 @@
     for j in range(LROWS):
         out[:, 128 * j : 128 * j + 128] = od[pl.ds(j, 4, stride=S), :]
 
-    for o in grp_offsets:
-        left(grp_peer(o), a_send, a_ss)
-        left(grp_peer(o), c_send, c_ss)
-    for o in wide_offsets:
-        left(wide_peer(o), t_send, t_ss)
-        left(wide_peer(o), l_send, l_ss)
-        left(wide_peer(o), f_send, f_ss)
+    for n, buf, sem in (
+        (ng - 1, a_send, a_ss), (ng - 1, c_send, c_ss), (nw - 1, t_send, t_ss), (nw - 1, l_send, l_ss), (nw - 1, f_send, f_ss),
+    ):
+        all_of(n, buf, sem)
 
 
 def per_device(dims, surf_depth, surf_color, surf_box, vol_color, vol_alpha, vol_box, ray_entry, ray_step, order):
@@ -293,13 +318,13 @@
     V, D = pltpu.VMEM, pltpu.SemaphoreType.DMA
     bf16 = jnp.bfloat16
     hbm = pl.BlockSpec(memory_space=pltpu.HBM)
-    smem = pl.BlockSpec(memory_space=pltpu.SMEM)
     frame = pl.pallas_call(
         functools.partial(kernel, dims),
-        out_shape=jax.ShapeDtypeStruct((4, PIX), F32),
-        in_specs=[hbm, hbm, smem, hbm, hbm, smem, hbm, hbm, smem],
+        out_shape=pltpu.VMEM((4, PIX), F32),
+        in_specs=[hbm] * 9,
         out_specs=pl.BlockSpec(memory_space=pltpu.VMEM),
         scratch_shapes=[
+            pltpu.SMEM((4, ng), I32), pltpu.SMEM((4, nw), I32), pltpu.SMEM((1, nw), I32),
             V((ng, PIX), I32), V((3, ng, PIX), bf16), V((nw, 3, SAMPLES, PIX), bf16), V((nw, SAMPLES, PIX), bf16),
             V((nw, PIX), I32), V((nw, PIX), I32),
             V((ng * S, 128), I32), V((3, ng * S, 128), F32), V((nw * S, 128), I32), V((nw * S, 128), I32),
@@ -311,10 +336,11 @@
             V((nw, 32, 128), I32), V((nw, 32, 128), I32),
             V((nw, SAMPLES, 16, 128), I32), V((nw, SAMPLES, 16, 128), I32),
             V((3, LROWS, 128), F32), V((4 * S, 128), F32),
-            D((6,)), D((ng,)), D((ng,)), D((ng,)), D((ng,)), D((nw,)), D((nw,)), D((nw,)), D((nw,)), D((nw,)), D((nw,)),
+            D((9,)), pltpu.SemaphoreType.REGULAR, pltpu.SemaphoreType.REGULAR,
+            D, D((2,)), D, D, D, D, D, D((nw,)), D, D,
         ],
         compiler_params=pltpu.CompilerParams(
-            collective_id=0, has_side_effects=True, vmem_limit_bytes=67043328
+            collective_id=0, has_side_effects=True, vmem_limit_bytes=66977792
         ),
     )(
         surf_depth[0, 0],

time: 29.6 us -> 24.7 us (0.83)
  the two profiles are of different devices: /device:TPU:1 before, /device:TPU:38 now
where the time goes in v2:
time: 24.7 us; the launch traced here: 24.6 us
  Pallas kernels  24 us (97%)
  local copies, waits for them, and re-layouts  0.63 us (3%)
    pallas_call x1, Pallas kernels, per_device(): pl.pallas_call(functools.partial(kernel, dims), out_shape=pltpu.VMEM((4,...  24 us
    unnamed x1, local copies, waits for them, and re-layouts  0.63 us

profile of v2, /device:TPU:38, one launch (start us, length us, event | category | flops | bytes accessed | tf_op | source)
XLA Modules:
  0.0 24.6 jit_solution(10116075236089986254)
XLA Ops:
  0.0 24.0 %shard_map.91 = f32[4,4096]{1,0:T(4,128)S(1)} custom-call(s32[16,4096]{1,0:T(8,128)} %bitcast.21, bf16[3,16,4096]{2,1,0:T(8,128)(2,1)} %bitcast.20, s32[4,16]{1,0:T(4,128)} %bitcast.24, bf16[16,3,8,4096]{3,2,1,0:T(8,128)(2,1)} %bitcast.18, bf16[16,8,4096]{2,1,0:T(8,128)(2,1)} %bitcast.19, s32[4,16]{1,0:T(4,128)} %bitcast.25, s32[16,4096]{1,0:T(8,128)} %bitcast.22, ...), custom_call_target="tpu_custom_call" | custom-call | tf_op jit(solution)/shard_map/pallas_call | solution.py:321
  24.0 0.6 %copy.11 = f32[1,1,4,4096]{3,2,1,0:T(4,128)} copy(f32[1,1,4,4096]{3,2,1,0:T(4,128)S(1)} %bitcast.17) | data formatting | bytes 131072

commit v3 on v2

--- a/solution.py
+++ b/solution.py
@@ -33,9 +33,9 @@
     sbox, vbox, order,
     sd_nat, sc_nat, vc_nat, va_nat, en_nat, st_nat,
     sd, sc, en, st, ad, cd,
-    a_send, a_recv, c_send, c_recv, t_send, t_recv, l_send, l_recv, f_send, f_recv,
+    a_send, a_recv, c_send, c_recv, l_send, l_recv, f_send, f_recv,
     tab0, tab1, surf, od,
-    lsem, g_ready, w_ready, a_ss, a_rs, c_ss, c_rs, t_ss, t_rs, l_ss, l_rs, f_ss, f_rs,
+    lsem, g_ready, w_ready, a_ss, a_rs, c_ss, c_rs, l_ss, l_rs, f_ss, f_rs,
 ):
     nx, ny, nz, ncore = dims
     nw, ng = nx * ny, nz * ncore
@@ -68,20 +68,19 @@
     half = ng // 2
     barrier = pltpu.get_barrier_semaphore()
 
-    def greet(sem_g, sem_w, wants):
+    def tell(sem, w, g):
+        pl.semaphore_signal(sem, inc=1, device_id=(w, g), device_id_type=MESH)
+
+    def tell_grp(sem, wants):
         for o in grp_offsets:
             peer = grp_peer(o)
-
-            @pl.when(wants(peer, me_g))
-            def _():
-                pl.semaphore_signal(sem_g, inc=1, device_id=(me_w, peer), device_id_type=MESH)
-
-        for o in wide_offsets:
-            peer = wide_peer(o)
-
-            @pl.when(wants(peer, me_w))
-            def _():
-                pl.semaphore_signal(sem_w, inc=1, device_id=(peer, me_g), device_id_type=MESH)
+            pl.when(wants(peer))(lambda peer=peer: tell(sem, me_w, peer))
+
+    def tell_plane(sem):
+        @pl.when(me_w == 0)
+        def _():
+            for o in wide_offsets:
+                tell(sem, wide_peer(o), me_g)
 
     loads = []
     for i, (src, dst) in enumerate(
@@ -93,7 +92,8 @@
         loads.append(pltpu.make_async_copy(src, dst, lsem.at[i]))
         if i < 4:
             loads[-1].start()
-    greet(barrier, barrier, lambda peer, me: peer > me)
+    tell_grp(barrier, lambda peer: peer > me_g)
+    tell_plane(barrier)
     for load in loads[4:]:
         load.start()
 
@@ -135,17 +135,19 @@
             folded = jnp.where(inside, sd[pl.ds(r * S + 8 * q, 8), :], folded)
         a_send[r, 0:8, :] = folded
         a_send[r, 8:9, :] = jnp.full((1, 128), sbox[0, r], I32)
-    loads[2].wait()
-    for c in range(nw):
-        t_send[c] = jnp.full((1, 128), vbox[0, c], I32)
     a_recv[me_g] = a_send[me_g]
-    t_recv[me_w] = t_send[me_w]
-
-    pl.when(me_g + me_w > 0)(lambda: pl.semaphore_wait(barrier, me_g + me_w))
-    greet(g_ready, w_ready, lambda peer, me: peer < me)
-
-    send_where(grp_offsets, grp_peer, me_g, grp_copy, lower, a_send, a_recv, a_ss, a_rs.at[me_g // half])
-    send_where(wide_offsets, wide_peer, me_w, wide_copy, lower, t_send, t_recv, t_ss, t_rs)
+
+    entered = me_g + (me_w > 0).astype(I32)
+    pl.when(entered > 0)(lambda: pl.semaphore_wait(barrier, entered))
+    tell_grp(g_ready, lambda peer: peer < me_g)
+    pl.when(me_w > 0)(lambda: tell(w_ready, 0, me_g))
+
+    def send_depths(wants):
+        for o in grp_offsets:
+            peer = grp_peer(o)
+            pl.when(wants(peer))(lambda peer=peer: grp_copy(peer, a_send, a_recv, a_ss, a_rs.at[me_g // half]).start())
+
+    send_depths(lambda peer: peer < me_g)
 
     loads[4].wait()
     for ch in range(3):
@@ -163,7 +165,7 @@
     lax.fori_loop(0, ng, fold_color, 0)
     c_recv[me_g] = c_send[me_g]
 
-    for load in loads[5:]:
+    for load in (loads[2], *loads[5:]):
         load.wait()
     spread(en_nat, en, nw)
     spread(st_nat, st, nw)
@@ -205,10 +207,13 @@
 
     lax.fori_loop(0, nw, prefixes, 0)
 
-    pl.when(me_w < nw - 1)(lambda: pl.semaphore_wait(w_ready, nw - 1 - me_w))
-    send_where(wide_offsets, wide_peer, me_w, wide_copy, higher, t_send, t_recv, t_ss, t_rs)
+    @pl.when(me_w == 0)
+    def _():
+        pl.semaphore_wait(w_ready, nw - 1)
+
+    tell_plane(w_ready)
     pl.when(me_g < ng - 1)(lambda: pl.semaphore_wait(g_ready, ng - 1 - me_g))
-    send_where(grp_offsets, grp_peer, me_g, grp_copy, higher, a_send, a_recv, a_ss, a_rs.at[me_g // half])
+    send_depths(lambda peer: peer > me_g)
 
     near = [jnp.full((8, 128), FAR, I32) for _ in range(4)]
     winner = [jnp.full((8, 128), -1, I32) for _ in range(4)]
@@ -225,18 +230,18 @@
             near[q] = jnp.where(take, depth, near[q])
             winner[q] = jnp.where(take, s, winner[q])
 
-    all_of(nw - 1, t_recv, t_rs)
-
     def upper_half(top):
         return (top + ((fold16 - top) & 31)) >= 32
 
-    near_lo = jnp.concatenate(near[:2], axis=0)
-    near_hi = jnp.concatenate(near[2:], axis=0)
-    for b in range(nw):
-        l_send[b] = jnp.where(upper_half(t_recv[b]), near_hi, near_lo)
-    l_recv[me_w] = l_send[me_w]
+    for q in range(4):
+        l_send[8 * q : 8 * q + 8, :] = near[q]
+    l_recv[me_w] = l_send[...]
+    pl.when(me_w > 0)(lambda: pl.semaphore_wait(w_ready, 1))
     for o in wide_offsets:
-        wide_copy(wide_peer(o), l_send, l_recv, l_ss, l_rs.at[me_w]).start()
+        pltpu.make_async_remote_copy(
+            src_ref=l_send, dst_ref=l_recv.at[me_w], send_sem=l_ss, recv_sem=l_rs.at[me_w],
+            device_id=(wide_peer(o), me_g), device_id_type=MESH,
+        ).start()
     for o in grp_offsets:
         grp_copy(grp_peer(o), c_send, c_recv, c_ss, c_rs).start()
 
@@ -249,7 +254,7 @@
 
     for c in by_start():
         pl.when(me_w != c)(lambda c=c: pltpu.make_async_copy(l_recv.at[c], l_recv.at[c], l_rs.at[c]).wait())
-        limit = l_recv[c]
+        limit = jnp.where(upper_half(vbox[0, c]), l_recv[c, 16:32, :], l_recv[c, 0:16, :])
         at = en[pl.ds(c * S, 16), :]
         stride = st[pl.ds(c * S, 16), :]
         word0 = jnp.zeros((16, 128), I32)
@@ -261,6 +266,7 @@
             at = at + stride
         f_send[c, 0:16, :] = word0
         f_send[c, 16:32, :] = word1
+        f_send[c, 32:33, :] = jnp.full((1, 128), vbox[0, c], I32)
 
         @pl.when(me_w != c)
         def _(c=c):
@@ -285,7 +291,7 @@
     for j in range(nw):
         b = order[0, j]
         word0, word1 = f_recv[b, 0:16, :], f_recv[b, 16:32, :]
-        upper = upper_half(t_recv[b])
+        upper = upper_half(f_recv[b, 32:33, :])
         layer = [
             lax.shift_right_logical(word0, 16).astype(F32),
             (word0 & 65535).astype(F32),
@@ -307,7 +313,7 @@
         out[:, 128 * j : 128 * j + 128] = od[pl.ds(j, 4, stride=S), :]
 
     for n, buf, sem in (
-        (ng - 1, a_send, a_ss), (ng - 1, c_send, c_ss), (nw - 1, t_send, t_ss), (nw - 1, l_send, l_ss), (nw - 1, f_send, f_ss),
+        (ng - 1, a_send, a_ss), (ng - 1, c_send, c_ss), (nw - 1, l_recv, l_ss), (nw - 1, f_send, f_ss),
     ):
         all_of(n, buf, sem)
 
@@ -331,13 +337,12 @@
             V((SAMPLES * S, 128), F32), V((3, SAMPLES * S, 128), F32),
             V((ng, 9, 128), I32), V((ng, 9, 128), I32),
             V((ng, 3, 8, 128), bf16), V((ng, 3, 8, 128), bf16),
-            V((nw, 1, 128), I32), V((nw, 1, 128), I32),
-            V((nw, 16, 128), I32), V((nw, 16, 128), I32),
-            V((nw, 32, 128), I32), V((nw, 32, 128), I32),
+            V((LROWS, 128), I32), V((nw, LROWS, 128), I32),
+            V((nw, 33, 128), I32), V((nw, 33, 128), I32),
             V((nw, SAMPLES, 16, 128), I32), V((nw, SAMPLES, 16, 128), I32),
             V((3, LROWS, 128), F32), V((4 * S, 128), F32),
             D((9,)), pltpu.SemaphoreType.REGULAR, pltpu.SemaphoreType.REGULAR,
-            D, D((2,)), D, D, D, D, D, D((nw,)), D, D,
+            D, D((2,)), D, D, D, D((nw,)), D, D,
         ],
         compiler_params=pltpu.CompilerParams(
             collective_id=0, has_side_effects=True, vmem_limit_bytes=66977792

time: 24.7 us -> 22.9 us (0.927)
  the two profiles are of different devices: /device:TPU:38 before, /device:TPU:6 now
where the time goes in v3:
time: 22.9 us; the launch traced here: 22.8 us
  Pallas kernels  22.2 us (97%)
  local copies, waits for them, and re-layouts  0.63 us (3%)
    pallas_call x1, Pallas kernels, per_device(): pl.pallas_call(functools.partial(kernel, dims), out_shape=pltpu.VMEM((4,...  22.2 us
    unnamed x1, local copies, waits for them, and re-layouts  0.63 us

profile of v3, /device:TPU:6, one launch (start us, length us, event | category | flops | bytes accessed | tf_op | source)
XLA Modules:
  0.0 22.8 jit_solution(465185092884150103)
XLA Ops:
  0.0 22.2 %shard_map.91 = f32[4,4096]{1,0:T(4,128)S(1)} custom-call(s32[16,4096]{1,0:T(8,128)} %bitcast.21, bf16[3,16,4096]{2,1,0:T(8,128)(2,1)} %bitcast.20, s32[4,16]{1,0:T(4,128)} %bitcast.24, bf16[16,3,8,4096]{3,2,1,0:T(8,128)(2,1)} %bitcast.18, bf16[16,8,4096]{2,1,0:T(8,128)(2,1)} %bitcast.19, s32[4,16]{1,0:T(4,128)} %bitcast.25, s32[16,4096]{1,0:T(8,128)} %bitcast.22, ...), custom_call_target="tpu_custom_call" | custom-call | tf_op jit(solution)/shard_map/pallas_call | solution.py:327
  22.2 0.6 %copy.11 = f32[1,1,4,4096]{3,2,1,0:T(4,128)} copy(f32[1,1,4,4096]{3,2,1,0:T(4,128)S(1)} %bitcast.17) | data formatting | bytes 131072

commit v4 on v2

--- a/solution.py
+++ b/solution.py
@@ -33,7 +33,7 @@
     sbox, vbox, order,
     sd_nat, sc_nat, vc_nat, va_nat, en_nat, st_nat,
     sd, sc, en, st, ad, cd,
-    a_send, a_recv, c_send, c_recv, t_send, t_recv, l_send, l_recv, f_send, f_recv,
+    a_send, a_recv, c_send, c_recv, t_send, t_recv, tops_of, l_full, l_send, l_recv, f_send, f_recv,
     tab0, tab1, surf, od,
     lsem, g_ready, w_ready, a_ss, a_rs, c_ss, c_rs, t_ss, t_rs, l_ss, l_rs, f_ss, f_rs,
 ):
@@ -66,22 +66,17 @@
         pltpu.make_async_copy(buf.at[pl.ds(0, n)], buf.at[pl.ds(0, n)], sem).wait()
 
     half = ng // 2
+    hub = jnp.where(me_g == 0, ny, 0)
+    late = (me_g >= half) & (me_g % 2 == 0)
     barrier = pltpu.get_barrier_semaphore()
 
-    def greet(sem_g, sem_w, wants):
+    def tell(sem, w, g):
+        pl.semaphore_signal(sem, inc=1, device_id=(w, g), device_id_type=MESH)
+
+    def tell_grp(sem, wants):
         for o in grp_offsets:
             peer = grp_peer(o)
-
-            @pl.when(wants(peer, me_g))
-            def _():
-                pl.semaphore_signal(sem_g, inc=1, device_id=(me_w, peer), device_id_type=MESH)
-
-        for o in wide_offsets:
-            peer = wide_peer(o)
-
-            @pl.when(wants(peer, me_w))
-            def _():
-                pl.semaphore_signal(sem_w, inc=1, device_id=(peer, me_g), device_id_type=MESH)
+            pl.when(wants(peer))(lambda peer=peer: tell(sem, me_w, peer))
 
     loads = []
     for i, (src, dst) in enumerate(
@@ -93,7 +88,13 @@
         loads.append(pltpu.make_async_copy(src, dst, lsem.at[i]))
         if i < 4:
             loads[-1].start()
-    greet(barrier, barrier, lambda peer, me: peer > me)
+    tell_grp(barrier, lambda peer: peer > me_g)
+
+    @pl.when(me_w == hub)
+    def _():
+        for o in wide_offsets:
+            tell(barrier, wide_peer(o), me_g)
+
     for load in loads[4:]:
         load.start()
 
@@ -119,6 +120,24 @@
                     tile = tile.astype(F32)
                 dense[pl.ds(h * g * S + j, g, stride=S), :] = tile
 
+    loads[2].wait()
+    tops = jnp.zeros((1, 128), I32)
+    for c in range(nw):
+        tops = jnp.where(lax.broadcasted_iota(I32, (1, 128), 1) == c, vbox[0, c], tops)
+    t_send[...] = tops
+    entered = me_g + (me_w != hub).astype(I32)
+    pl.when(entered > 0)(lambda: pl.semaphore_wait(barrier, entered))
+    tell_grp(g_ready, lambda peer: peer < me_g)
+
+    @pl.when(me_w != hub)
+    def _():
+        pltpu.make_async_remote_copy(
+            src_ref=t_send, dst_ref=t_recv.at[me_w], send_sem=t_ss, recv_sem=t_rs,
+            device_id=(hub, me_g), device_id_type=MESH,
+        ).start()
+
+    pl.when(late & (me_w != hub))(lambda: tell(w_ready, hub, me_g))
+
     loads[0].wait()
     loads[1].wait()
     spread(sd_nat, sd, ng)
@@ -128,6 +147,12 @@
         return [
             inx & (fold8 + 16 * q >= sbox[0, r]) & (fold8 + 16 * q < sbox[1, r]) for q in range(4)
         ]
+
+    def send_depth(peer, wanted):
+        pl.when(wanted)(lambda: grp_copy(peer, a_send, a_recv, a_ss, a_rs.at[me_g // half]).start())
+
+    def send_color(peer, wanted):
+        pl.when(wanted)(lambda: grp_copy(peer, c_send, c_recv, c_ss, c_rs).start())
 
     for r in range(ng):
         folded = jnp.full((8, 128), FAR, I32)
@@ -135,17 +160,9 @@
             folded = jnp.where(inside, sd[pl.ds(r * S + 8 * q, 8), :], folded)
         a_send[r, 0:8, :] = folded
         a_send[r, 8:9, :] = jnp.full((1, 128), sbox[0, r], I32)
-    loads[2].wait()
-    for c in range(nw):
-        t_send[c] = jnp.full((1, 128), vbox[0, c], I32)
+        if r:
+            send_depth(r - 1, r - 1 < me_g)
     a_recv[me_g] = a_send[me_g]
-    t_recv[me_w] = t_send[me_w]
-
-    pl.when(me_g + me_w > 0)(lambda: pl.semaphore_wait(barrier, me_g + me_w))
-    greet(g_ready, w_ready, lambda peer, me: peer < me)
-
-    send_where(grp_offsets, grp_peer, me_g, grp_copy, lower, a_send, a_recv, a_ss, a_rs.at[me_g // half])
-    send_where(wide_offsets, wide_peer, me_w, wide_copy, lower, t_send, t_recv, t_ss, t_rs)
 
     loads[4].wait()
     for ch in range(3):
@@ -205,10 +222,29 @@
 
     lax.fori_loop(0, nw, prefixes, 0)
 
-    pl.when(me_w < nw - 1)(lambda: pl.semaphore_wait(w_ready, nw - 1 - me_w))
-    send_where(wide_offsets, wide_peer, me_w, wide_copy, higher, t_send, t_recv, t_ss, t_rs)
+    def pass_tops():
+        all_of(nw - 1, t_recv, t_rs)
+        t_recv[hub] = t_send[...]
+        for o in wide_offsets:
+            pltpu.make_async_remote_copy(
+                src_ref=t_recv, dst_ref=t_recv, send_sem=t_ss, recv_sem=t_rs,
+                device_id=(wide_peer(o), me_g), device_id_type=MESH,
+            ).start()
+
+    pl.when((me_w == hub) & (me_g < ncore))(pass_tops)
+    for o in grp_offsets:
+        send_color(grp_peer(o), grp_peer(o) < me_g)
     pl.when(me_g < ng - 1)(lambda: pl.semaphore_wait(g_ready, ng - 1 - me_g))
-    send_where(grp_offsets, grp_peer, me_g, grp_copy, higher, a_send, a_recv, a_ss, a_rs.at[me_g // half])
+    for o in grp_offsets:
+        send_depth(grp_peer(o), grp_peer(o) > me_g)
+
+    pl.when((me_w == hub) & (me_g >= ncore) & jnp.logical_not(late))(pass_tops)
+
+    @pl.when((me_w == hub) & late)
+    def _():
+        pl.semaphore_wait(w_ready, nw - 1)
+        for o in wide_offsets:
+            tell(w_ready, wide_peer(o), me_g)
 
     near = [jnp.full((8, 128), FAR, I32) for _ in range(4)]
     winner = [jnp.full((8, 128), -1, I32) for _ in range(4)]
@@ -225,20 +261,45 @@
             near[q] = jnp.where(take, depth, near[q])
             winner[q] = jnp.where(take, s, winner[q])
 
-    all_of(nw - 1, t_recv, t_rs)
-
     def upper_half(top):
         return (top + ((fold16 - top) & 31)) >= 32
 
+    def take_tops():
+        pl.when(me_w != hub)(lambda: all_of(nw, t_recv, t_rs))
+        for b in range(nw):
+            mine = jnp.where(lax.broadcasted_iota(I32, (1, 128), 1) == me_w, t_recv[b], 0).astype(F32)
+            tops_of[b] = jnp.broadcast_to(jnp.sum(mine, axis=1, keepdims=True), (1, 128)).astype(I32)
+
+    def limit_copy(peer, src, rows):
+        return pltpu.make_async_remote_copy(
+            src_ref=src, dst_ref=l_recv.at[me_w, pl.ds(0, rows)], send_sem=l_ss, recv_sem=l_rs.at[me_w],
+            device_id=(peer, me_g), device_id_type=MESH,
+        )
+
     near_lo = jnp.concatenate(near[:2], axis=0)
     near_hi = jnp.concatenate(near[2:], axis=0)
-    for b in range(nw):
-        l_send[b] = jnp.where(upper_half(t_recv[b]), near_hi, near_lo)
-    l_recv[me_w] = l_send[me_w]
-    for o in wide_offsets:
-        wide_copy(wide_peer(o), l_send, l_recv, l_ss, l_rs.at[me_w]).start()
+    l_full[0:16, :] = near_lo
+    l_full[16:32, :] = near_hi
+
+    @pl.when(late)
+    def _():
+        l_recv[me_w] = l_full[...]
+        pl.when(me_w != hub)(lambda: pl.semaphore_wait(w_ready, 1))
+        for o in wide_offsets:
+            limit_copy(wide_peer(o), l_full, LROWS).start()
+
+    @pl.when(jnp.logical_not(late))
+    def _():
+        take_tops()
+        for o in [*wide_offsets, (0, 0)]:
+            l_send[wide_peer(o)] = jnp.where(upper_half(tops_of[wide_peer(o)]), l_full[16:32, :], l_full[0:16, :])
+        l_recv[me_w, 0:16, :] = l_send[me_w]
+        for o in wide_offsets:
+            limit_copy(wide_peer(o), l_send.at[wide_peer(o)], 16).start()
+
     for o in grp_offsets:
-        grp_copy(grp_peer(o), c_send, c_recv, c_ss, c_rs).start()
+        send_color(grp_peer(o), grp_peer(o) > me_g)
+    pl.when((me_w == hub) & late)(pass_tops)
 
     def by_start():
         for k in range(nx + ny - 1):
@@ -248,8 +309,10 @@
                 yield x * ny + k - x
 
     for c in by_start():
-        pl.when(me_w != c)(lambda c=c: pltpu.make_async_copy(l_recv.at[c], l_recv.at[c], l_rs.at[c]).wait())
-        limit = l_recv[c]
+        for rows, here in ((LROWS, late), (16, jnp.logical_not(late))):
+            part = l_recv.at[c, pl.ds(0, rows)]
+            pl.when((me_w != c) & here)(lambda c=c, part=part: pltpu.make_async_copy(part, part, l_rs.at[c]).wait())
+        limit = jnp.where(late & upper_half(vbox[0, c]), l_recv[c, 16:32, :], l_recv[c, 0:16, :])
         at = en[pl.ds(c * S, 16), :]
         stride = st[pl.ds(c * S, 16), :]
         word0 = jnp.zeros((16, 128), I32)
@@ -267,6 +330,7 @@
             wide_copy(c, f_send, f_recv, f_ss, f_rs).start()
 
     f_recv[me_w] = f_send[me_w]
+    pl.when(late)(take_tops)
     all_of(ng - 1, c_recv, c_rs)
     color = [[jnp.zeros((8, 128), F32) for _ in range(3)] for _ in range(4)]
     for s in range(ng):
@@ -285,7 +349,7 @@
     for j in range(nw):
         b = order[0, j]
         word0, word1 = f_recv[b, 0:16, :], f_recv[b, 16:32, :]
-        upper = upper_half(t_recv[b])
+        upper = upper_half(tops_of[b])
         layer = [
             lax.shift_right_logical(word0, 16).astype(F32),
             (word0 & 65535).astype(F32),
@@ -307,9 +371,21 @@
         out[:, 128 * j : 128 * j + 128] = od[pl.ds(j, 4, stride=S), :]
 
     for n, buf, sem in (
-        (ng - 1, a_send, a_ss), (ng - 1, c_send, c_ss), (nw - 1, t_send, t_ss), (nw - 1, l_send, l_ss), (nw - 1, f_send, f_ss),
+        (ng - 1, a_send, a_ss), (ng - 1, c_send, c_ss), (nw - 1, f_send, f_ss),
     ):
         all_of(n, buf, sem)
+
+    pl.when(late)(lambda: all_of(nw - 1, l_recv, l_ss))
+    pl.when(jnp.logical_not(late))(lambda: all_of(nw - 1, l_send, l_ss))
+
+    @pl.when(me_w != hub)
+    def _():
+        pltpu.make_async_copy(t_send, t_send, t_ss).wait()
+
+    @pl.when(me_w == hub)
+    def _():
+        for o in wide_offsets:
+            all_of(nw, t_recv, t_ss)
 
 
 def per_device(dims, surf_depth, surf_color, surf_box, vol_color, vol_alpha, vol_box, ray_entry, ray_step, order):
@@ -331,9 +407,9 @@
             V((SAMPLES * S, 128), F32), V((3, SAMPLES * S, 128), F32),
             V((ng, 9, 128), I32), V((ng, 9, 128), I32),
             V((ng, 3, 8, 128), bf16), V((ng, 3, 8, 128), bf16),
-            V((nw, 1, 128), I32), V((nw, 1, 128), I32),
-            V((nw, 16, 128), I32), V((nw, 16, 128), I32),
-            V((nw, 32, 128), I32), V((nw, 32, 128), I32),
+            V((1, 128), I32), V((nw, 1, 128), I32), V((nw, 1, 128), I32),
+            V((LROWS, 128), I32), V((nw, 16, 128), I32), V((nw, LROWS, 128), I32),
+            V((nw, LROWS, 128), I32), V((nw, LROWS, 128), I32),
             V((nw, SAMPLES, 16, 128), I32), V((nw, SAMPLES, 16, 128), I32),
             V((3, LROWS, 128), F32), V((4 * S, 128), F32),
             D((9,)), pltpu.SemaphoreType.REGULAR, pltpu.SemaphoreType.REGULAR,

time: 24.7 us -> 22.3 us (0.903)
  the two profiles are of different devices: /device:TPU:38 before, /device:TPU:230 now
where the time goes in v4:
time: 22.3 us; the launch traced here: 22.1 us
  Pallas kernels  21.5 us (96%)
  local copies, waits for them, and re-layouts  0.63 us (3%)
    pallas_call x1, Pallas kernels, per_device(): pl.pallas_call(functools.partial(kernel, dims), out_shape=pltpu.VMEM((4,...  21.5 us
    unnamed x1, local copies, waits for them, and re-layouts  0.63 us

profile of v4, /device:TPU:230, one launch (start us, length us, event | category | flops | bytes accessed | tf_op | source)
XLA Modules:
  0.0 22.1 jit_solution(14253910640234165341)
XLA Ops:
  0.0 21.5 %shard_map.91 = f32[4,4096]{1,0:T(4,128)S(1)} custom-call(s32[16,4096]{1,0:T(8,128)} %bitcast.21, bf16[3,16,4096]{2,1,0:T(8,128)(2,1)} %bitcast.20, s32[4,16]{1,0:T(4,128)} %bitcast.24, bf16[16,3,8,4096]{3,2,1,0:T(8,128)(2,1)} %bitcast.18, bf16[16,8,4096]{2,1,0:T(8,128)(2,1)} %bitcast.19, s32[4,16]{1,0:T(4,128)} %bitcast.25, s32[16,4096]{1,0:T(8,128)} %bitcast.22, ...), custom_call_target="tpu_custom_call" | custom-call | tf_op jit(solution)/shard_map/pallas_call | solution.py:397
  21.5 0.6 %copy.11 = f32[1,1,4,4096]{3,2,1,0:T(4,128)} copy(f32[1,1,4,4096]{3,2,1,0:T(4,128)S(1)} %bitcast.17) | data formatting | bytes 131072

commit v5 on v2

--- a/solution.py
+++ b/solution.py
@@ -33,9 +33,9 @@
     sbox, vbox, order,
     sd_nat, sc_nat, vc_nat, va_nat, en_nat, st_nat,
     sd, sc, en, st, ad, cd,
-    a_send, a_recv, c_send, c_recv, t_send, t_recv, l_send, l_recv, f_send, f_recv,
+    a_send, a_recv, c_send, c_recv, t_send, t_hub, t_recv, tops_of, l_send, l_recv, f_send, f_recv,
     tab0, tab1, surf, od,
-    lsem, g_ready, w_ready, a_ss, a_rs, c_ss, c_rs, t_ss, t_rs, l_ss, l_rs, f_ss, f_rs,
+    lsem, g_ready, a_ss, a_rs, c_ss, c_rs, t_ss, h_rs, t_rs, l_ss, l_rs, f_ss, f_rs,
 ):
     nx, ny, nz, ncore = dims
     nw, ng = nx * ny, nz * ncore
@@ -66,22 +66,19 @@
         pltpu.make_async_copy(buf.at[pl.ds(0, n)], buf.at[pl.ds(0, n)], sem).wait()
 
     half = ng // 2
+    core = me_g % ncore
+    first_g = me_g // ncore * ncore
+    hub_g = first_g + ncore - 1
+    is_hub = (me_w == 0) & (me_g == hub_g)
     barrier = pltpu.get_barrier_semaphore()
 
-    def greet(sem_g, sem_w, wants):
+    def tell(sem, w, g):
+        pl.semaphore_signal(sem, inc=1, device_id=(w, g), device_id_type=MESH)
+
+    def tell_grp(sem, wants):
         for o in grp_offsets:
             peer = grp_peer(o)
-
-            @pl.when(wants(peer, me_g))
-            def _():
-                pl.semaphore_signal(sem_g, inc=1, device_id=(me_w, peer), device_id_type=MESH)
-
-        for o in wide_offsets:
-            peer = wide_peer(o)
-
-            @pl.when(wants(peer, me_w))
-            def _():
-                pl.semaphore_signal(sem_w, inc=1, device_id=(peer, me_g), device_id_type=MESH)
+            pl.when(wants(peer))(lambda peer=peer: tell(sem, me_w, peer))
 
     loads = []
     for i, (src, dst) in enumerate(
@@ -93,7 +90,18 @@
         loads.append(pltpu.make_async_copy(src, dst, lsem.at[i]))
         if i < 4:
             loads[-1].start()
-    greet(barrier, barrier, lambda peer, me: peer > me)
+    tell_grp(barrier, lambda peer: peer > me_g)
+
+    def planes(act):
+        for k in range(ncore):
+            for w in range(nw):
+                if (k, w) != (ncore - 1, 0):
+                    act(k, w)
+
+    @pl.when(is_hub)
+    def _():
+        planes(lambda k, w: tell(barrier, w, first_g + k))
+
     for load in loads[4:]:
         load.start()
 
@@ -119,6 +127,24 @@
                     tile = tile.astype(F32)
                 dense[pl.ds(h * g * S + j, g, stride=S), :] = tile
 
+    loads[2].wait()
+    tops = jnp.zeros((1, 128), I32)
+    for c in range(nw):
+        tops = jnp.where(lax.broadcasted_iota(I32, (1, 128), 1) == c, vbox[0, c], tops)
+    t_send[...] = tops
+    entered = me_g + jnp.logical_not(is_hub).astype(I32)
+    pl.when(entered > 0)(lambda: pl.semaphore_wait(barrier, entered))
+    tell_grp(g_ready, lambda peer: peer < me_g)
+
+    for k in range(ncore):
+
+        @pl.when((core == k) & jnp.logical_not(is_hub))
+        def _(k=k):
+            pltpu.make_async_remote_copy(
+                src_ref=t_send, dst_ref=t_hub.at[k, me_w], send_sem=t_ss, recv_sem=h_rs.at[k],
+                device_id=(0, hub_g), device_id_type=MESH,
+            ).start()
+
     loads[0].wait()
     loads[1].wait()
     spread(sd_nat, sd, ng)
@@ -128,6 +154,12 @@
         return [
             inx & (fold8 + 16 * q >= sbox[0, r]) & (fold8 + 16 * q < sbox[1, r]) for q in range(4)
         ]
+
+    def send_depth(peer, wanted):
+        pl.when(wanted)(lambda: grp_copy(peer, a_send, a_recv, a_ss, a_rs.at[me_g // half]).start())
+
+    def send_color(peer, wanted):
+        pl.when(wanted)(lambda: grp_copy(peer, c_send, c_recv, c_ss, c_rs).start())
 
     for r in range(ng):
         folded = jnp.full((8, 128), FAR, I32)
@@ -135,17 +167,9 @@
             folded = jnp.where(inside, sd[pl.ds(r * S + 8 * q, 8), :], folded)
         a_send[r, 0:8, :] = folded
         a_send[r, 8:9, :] = jnp.full((1, 128), sbox[0, r], I32)
-    loads[2].wait()
-    for c in range(nw):
-        t_send[c] = jnp.full((1, 128), vbox[0, c], I32)
+        if r:
+            send_depth(r - 1, r - 1 < me_g)
     a_recv[me_g] = a_send[me_g]
-    t_recv[me_w] = t_send[me_w]
-
-    pl.when(me_g + me_w > 0)(lambda: pl.semaphore_wait(barrier, me_g + me_w))
-    greet(g_ready, w_ready, lambda peer, me: peer < me)
-
-    send_where(grp_offsets, grp_peer, me_g, grp_copy, lower, a_send, a_recv, a_ss, a_rs.at[me_g // half])
-    send_where(wide_offsets, wide_peer, me_w, wide_copy, lower, t_send, t_recv, t_ss, t_rs)
 
     loads[4].wait()
     for ch in range(3):
@@ -205,10 +229,27 @@
 
     lax.fori_loop(0, nw, prefixes, 0)
 
-    pl.when(me_w < nw - 1)(lambda: pl.semaphore_wait(w_ready, nw - 1 - me_w))
-    send_where(wide_offsets, wide_peer, me_w, wide_copy, higher, t_send, t_recv, t_ss, t_rs)
+    def pass_tops():
+        for k in reversed(range(ncore)):
+            all_of(nw - 1 if k == ncore - 1 else nw, t_hub.at[k], h_rs.at[k])
+            if k == ncore - 1:
+                t_hub[k, 0] = t_send[...]
+                t_recv[...] = t_hub[k]
+            for w in range(nw):
+                if (k, w) != (ncore - 1, 0):
+                    pltpu.make_async_remote_copy(
+                        src_ref=t_hub.at[k], dst_ref=t_recv, send_sem=t_ss, recv_sem=t_rs,
+                        device_id=(w, first_g + k), device_id_type=MESH,
+                    ).start()
+
+    pl.when(is_hub & (me_g < ncore))(pass_tops)
+    for o in grp_offsets:
+        send_color(grp_peer(o), grp_peer(o) < me_g)
     pl.when(me_g < ng - 1)(lambda: pl.semaphore_wait(g_ready, ng - 1 - me_g))
-    send_where(grp_offsets, grp_peer, me_g, grp_copy, higher, a_send, a_recv, a_ss, a_rs.at[me_g // half])
+    for o in grp_offsets:
+        send_depth(grp_peer(o), grp_peer(o) > me_g)
+
+    pl.when(is_hub & (me_g >= ncore))(pass_tops)
 
     near = [jnp.full((8, 128), FAR, I32) for _ in range(4)]
     winner = [jnp.full((8, 128), -1, I32) for _ in range(4)]
@@ -225,20 +266,22 @@
             near[q] = jnp.where(take, depth, near[q])
             winner[q] = jnp.where(take, s, winner[q])
 
-    all_of(nw - 1, t_recv, t_rs)
-
     def upper_half(top):
         return (top + ((fold16 - top) & 31)) >= 32
 
     near_lo = jnp.concatenate(near[:2], axis=0)
     near_hi = jnp.concatenate(near[2:], axis=0)
+    pl.when(jnp.logical_not(is_hub))(lambda: all_of(nw, t_recv, t_rs))
     for b in range(nw):
-        l_send[b] = jnp.where(upper_half(t_recv[b]), near_hi, near_lo)
+        mine = jnp.where(lax.broadcasted_iota(I32, (1, 128), 1) == me_w, t_recv[b], 0).astype(F32)
+        tops_of[b] = jnp.broadcast_to(jnp.sum(mine, axis=1, keepdims=True), (1, 128)).astype(I32)
+    for o in [*wide_offsets, (0, 0)]:
+        l_send[wide_peer(o)] = jnp.where(upper_half(tops_of[wide_peer(o)]), near_hi, near_lo)
     l_recv[me_w] = l_send[me_w]
     for o in wide_offsets:
         wide_copy(wide_peer(o), l_send, l_recv, l_ss, l_rs.at[me_w]).start()
     for o in grp_offsets:
-        grp_copy(grp_peer(o), c_send, c_recv, c_ss, c_rs).start()
+        send_color(grp_peer(o), grp_peer(o) > me_g)
 
     def by_start():
         for k in range(nx + ny - 1):
@@ -285,7 +328,7 @@
     for j in range(nw):
         b = order[0, j]
         word0, word1 = f_recv[b, 0:16, :], f_recv[b, 16:32, :]
-        upper = upper_half(t_recv[b])
+        upper = upper_half(tops_of[b])
         layer = [
             lax.shift_right_logical(word0, 16).astype(F32),
             (word0 & 65535).astype(F32),
@@ -307,9 +350,15 @@
         out[:, 128 * j : 128 * j + 128] = od[pl.ds(j, 4, stride=S), :]
 
     for n, buf, sem in (
-        (ng - 1, a_send, a_ss), (ng - 1, c_send, c_ss), (nw - 1, t_send, t_ss), (nw - 1, l_send, l_ss), (nw - 1, f_send, f_ss),
+        (ng - 1, a_send, a_ss), (ng - 1, c_send, c_ss), (nw - 1, l_send, l_ss), (nw - 1, f_send, f_ss),
     ):
         all_of(n, buf, sem)
+
+    pl.when(jnp.logical_not(is_hub))(lambda: pltpu.make_async_copy(t_send, t_send, t_ss).wait())
+
+    @pl.when(is_hub)
+    def _():
+        planes(lambda k, w: all_of(nw, t_recv, t_ss))
 
 
 def per_device(dims, surf_depth, surf_color, surf_box, vol_color, vol_alpha, vol_box, ray_entry, ray_step, order):
@@ -331,13 +380,13 @@
             V((SAMPLES * S, 128), F32), V((3, SAMPLES * S, 128), F32),
             V((ng, 9, 128), I32), V((ng, 9, 128), I32),
             V((ng, 3, 8, 128), bf16), V((ng, 3, 8, 128), bf16),
-            V((nw, 1, 128), I32), V((nw, 1, 128), I32),
+            V((1, 128), I32), V((ncore, nw, 1, 128), I32), V((nw, 1, 128), I32), V((nw, 1, 128), I32),
             V((nw, 16, 128), I32), V((nw, 16, 128), I32),
-            V((nw, 32, 128), I32), V((nw, 32, 128), I32),
+            V((nw, LROWS, 128), I32), V((nw, LROWS, 128), I32),
             V((nw, SAMPLES, 16, 128), I32), V((nw, SAMPLES, 16, 128), I32),
             V((3, LROWS, 128), F32), V((4 * S, 128), F32),
-            D((9,)), pltpu.SemaphoreType.REGULAR, pltpu.SemaphoreType.REGULAR,
-            D, D((2,)), D, D, D, D, D, D((nw,)), D, D,
+            D((9,)), pltpu.SemaphoreType.REGULAR,
+            D, D((2,)), D, D, D, D((ncore,)), D, D, D((nw,)), D, D,
         ],
         compiler_params=pltpu.CompilerParams(
             collective_id=0, has_side_effects=True, vmem_limit_bytes=66977792

time: 24.7 us -> 22.3 us (0.903)
  the two profiles are of different devices: /device:TPU:38 before, /device:TPU:230 now
where the time goes in v5:
time: 22.3 us; the launch traced here: 22.2 us
  Pallas kernels  21.6 us (97%)
  local copies, waits for them, and re-layouts  0.63 us (3%)
    pallas_call x1, Pallas kernels, per_device(): pl.pallas_call(functools.partial(kernel, dims), out_shape=pltpu.VMEM((4,...  21.6 us
    unnamed x1, local copies, waits for them, and re-layouts  0.63 us

profile of v5, /device:TPU:230, one launch (start us, length us, event | category | flops | bytes accessed | tf_op | source)
XLA Modules:
  0.0 22.2 jit_solution(16697052307359911025)
XLA Ops:
  0.0 21.6 %shard_map.91 = f32[4,4096]{1,0:T(4,128)S(1)} custom-call(s32[16,4096]{1,0:T(8,128)} %bitcast.21, bf16[3,16,4096]{2,1,0:T(8,128)(2,1)} %bitcast.20, s32[4,16]{1,0:T(4,128)} %bitcast.24, bf16[16,3,8,4096]{3,2,1,0:T(8,128)(2,1)} %bitcast.18, bf16[16,8,4096]{2,1,0:T(8,128)(2,1)} %bitcast.19, s32[4,16]{1,0:T(4,128)} %bitcast.25, s32[16,4096]{1,0:T(8,128)} %bitcast.22, ...), custom_call_target="tpu_custom_call" | custom-call | tf_op jit(solution)/shard_map/pallas_call | solution.py:370
  21.6 0.6 %copy.11 = f32[1,1,4,4096]{3,2,1,0:T(4,128)} copy(f32[1,1,4,4096]{3,2,1,0:T(4,128)S(1)} %bitcast.17) | data formatting | bytes 131072

commit v6 on v5

--- a/solution.py
+++ b/solution.py
@@ -251,9 +251,17 @@
 
     pl.when(is_hub & (me_g >= ncore))(pass_tops)
 
+    def take_tops():
+        pl.when(jnp.logical_not(is_hub))(lambda: all_of(nw, t_recv, t_rs))
+        for b in range(nw):
+            mine = jnp.where(lax.broadcasted_iota(I32, (1, 128), 1) == me_w, t_recv[b], 0).astype(F32)
+            tops_of[b] = jnp.broadcast_to(jnp.sum(mine, axis=1, keepdims=True), (1, 128)).astype(I32)
+
     near = [jnp.full((8, 128), FAR, I32) for _ in range(4)]
     winner = [jnp.full((8, 128), -1, I32) for _ in range(4)]
     for s in range(ng):
+        if s == half:
+            take_tops()
         if s % half == 0:
             own = me_g // half == s // half
             pl.when(own)(lambda: all_of(half - 1, a_recv, a_rs.at[s // half]))
@@ -271,10 +279,6 @@
 
     near_lo = jnp.concatenate(near[:2], axis=0)
     near_hi = jnp.concatenate(near[2:], axis=0)
-    pl.when(jnp.logical_not(is_hub))(lambda: all_of(nw, t_recv, t_rs))
-    for b in range(nw):
-        mine = jnp.where(lax.broadcasted_iota(I32, (1, 128), 1) == me_w, t_recv[b], 0).astype(F32)
-        tops_of[b] = jnp.broadcast_to(jnp.sum(mine, axis=1, keepdims=True), (1, 128)).astype(I32)
     for o in [*wide_offsets, (0, 0)]:
         l_send[wide_peer(o)] = jnp.where(upper_half(tops_of[wide_peer(o)]), near_hi, near_lo)
     l_recv[me_w] = l_send[me_w]

time: 22.3 us -> 22.3 us (level)
  no operation moved by 1% of the time
where the time goes in v6:
time: 22.3 us
  Pallas kernels  21.6 us (97%)
  local copies, waits for them, and re-layouts  0.63 us (3%)
    pallas_call x1, Pallas kernels, per_device(): pl.pallas_call(functools.partial(kernel, dims), out_shape=pltpu.VMEM((4,...  21.6 us
    unnamed x1, local copies, waits for them, and re-layouts  0.63 us

profile of v6, /device:TPU:230, one launch (start us, length us, event | category | flops | bytes accessed | tf_op | source)
XLA Modules:
  0.0 22.3 jit_solution(6888546482838136878)
XLA Ops:
  0.0 21.6 %shard_map.91 = f32[4,4096]{1,0:T(4,128)S(1)} custom-call(s32[16,4096]{1,0:T(8,128)} %bitcast.21, bf16[3,16,4096]{2,1,0:T(8,128)(2,1)} %bitcast.20, s32[4,16]{1,0:T(4,128)} %bitcast.24, bf16[16,3,8,4096]{3,2,1,0:T(8,128)(2,1)} %bitcast.18, bf16[16,8,4096]{2,1,0:T(8,128)(2,1)} %bitcast.19, s32[4,16]{1,0:T(4,128)} %bitcast.25, s32[16,4096]{1,0:T(8,128)} %bitcast.22, ...), custom_call_target="tpu_custom_call" | custom-call | tf_op jit(solution)/shard_map/pallas_call | solution.py:374
  21.6 0.6 %copy.11 = f32[1,1,4,4096]{3,2,1,0:T(4,128)} copy(f32[1,1,4,4096]{3,2,1,0:T(4,128)S(1)} %bitcast.17) | data formatting | bytes 131072
